TPU v7x, 128 devices: a whole 4x4x4 slice. The times are simulated.
128 devices in a mesh: section: 8 (over y_hi, z), dp: 16 (over x, y_lo, core).
Axes of the slice: x: 4, y: 4 (y_hi: 2, y_lo: 2; y = y_hi * 2 + y_lo), z: 4, core: 2. Of those that a mesh axis runs over, the one named last changes fastest.
Arguments:
- activations: bfloat16 [8, 4, 4096, 1280], P('section', None, 'dp'), may hold values from -6 to 6
- cotangent: bfloat16 [4, 4096, 1280], P(None, 'dp'), may hold values from -1.5 to 1.5
- counts: int32 [4, 16], P(None, 'dp'), may hold values from 64 to 256
- arrival: int32 [4], replicated, may hold values from 0 to 3, each once
- norm_gain: float32 [8, 1280], P('section'), may hold values from 0.1 to 1.9
- qkv_weight: bfloat16 [8, 1280, 1920], P('section'), may hold values from -8 to 8
- out_weight: bfloat16 [8, 1280, 640], P('section'), may hold values from -0.25 to 0.25
Outputs:
- qkv_grad: float32 [8, 1280, 1920], P('section', 'dp')
- out_grad: float32 [8, 1280, 640], P('section', 'dp')
Inputs may be any that keep to these rules, and one draw needn't show every extreme that they name: `arrival`: each microbatch once.
All inputs are finite; a program needn't handle non-finite values.
Results may differ from a plain program's by a relative error of at most 0.025.
Values may be sent and summed in bfloat16 or wider, within the bound.
A program may use at most 128 MiB of HBM per device.

v0:
```python
import jax
import jax.numpy as jnp
from jax import lax
from jax.sharding import PartitionSpec as P

HDIM = 80
HEADS = 8


EPSILON = 1e-06


def shifted(value, axis, steps):
    count = lax.axis_size(axis)
    initial, last = (max(0, -steps), min(count, count - steps))
    return lax.ppermute(value, axis, [(source, source + steps) for source in range(initial, last)])


def in_one_piece(arrays, axis, dim, along):
    ends, at = ([], 0)
    for a in arrays[:-1]:
        at += a.shape[along]
        ends.append(at)
    both = jnp.concatenate(arrays, axis=along)
    return tuple(
        jnp.split(lax.psum_scatter(both, axis, scatter_dimension=dim, tiled=True), ends, axis=along)
    )


def cross(left, right):
    return lax.dot_general(
        left, right, (((0,), (0,)), ((), ())), preferred_element_type=jnp.float32
    )


def backward_layer(inputs, grad_out, visible, gain_row, w_qkv, w_out):
    slot_count = inputs.shape[0]
    floats = inputs.astype(jnp.float32)
    centered = floats - jnp.mean(floats, axis=-1, keepdims=True)
    inv_std = lax.rsqrt(jnp.mean(centered * centered, axis=-1, keepdims=True) + EPSILON)
    normed = centered * inv_std
    hidden = (normed * gain_row).astype(jnp.bfloat16)
    packed = jnp.dot(hidden, w_qkv, preferred_element_type=jnp.float32).astype(jnp.bfloat16)
    head_span = packed.shape[1] // 3
    queries = packed[:, :head_span].reshape(slot_count, HEADS, HDIM)
    keys_all = packed[:, head_span : 2 * head_span].reshape(slot_count, HEADS, HDIM)
    values_all = packed[:, 2 * head_span :].reshape(slot_count, HEADS, HDIM)
    scores = jnp.einsum(
        "ihd,jhd->hij", queries, keys_all, preferred_element_type=jnp.float32
    ) * HDIM ** (-0.5)
    keep = jnp.arange(slot_count) < visible
    scores = jnp.where(keep[None, None, :], scores, -1e30)
    row_max = jnp.max(scores, axis=-1, keepdims=True)
    exp_scores = jnp.exp(scores - row_max)
    prob_full = exp_scores / jnp.sum(exp_scores, axis=-1, keepdims=True)
    prob_half = prob_full.astype(jnp.bfloat16)
    attn_out = jnp.einsum("hij,jhd->ihd", prob_half, values_all, preferred_element_type=jnp.float32)
    attn_out = attn_out.reshape(slot_count, head_span).astype(jnp.bfloat16)
    masked = jnp.where(keep[:, None], grad_out, jnp.zeros_like(grad_out))
    grad_attn = jnp.dot(masked, w_out, preferred_element_type=jnp.float32).astype(jnp.bfloat16)
    grad_attn = grad_attn.reshape(slot_count, HEADS, HDIM)
    grad_prob = jnp.einsum(
        "ihd,jhd->hij", grad_attn, values_all, preferred_element_type=jnp.float32
    )
    grad_values = jnp.einsum(
        "hij,ihd->jhd", prob_half, grad_attn, preferred_element_type=jnp.float32
    )
    inner = jnp.sum(prob_full * grad_prob, axis=-1, keepdims=True)
    grad_scores = (prob_full * (grad_prob - inner) * HDIM ** (-0.5)).astype(jnp.bfloat16)
    grad_queries = jnp.einsum(
        "hij,jhd->ihd", grad_scores, keys_all, preferred_element_type=jnp.float32
    )
    grad_keys = jnp.einsum("hij,ihd->jhd", grad_scores, queries, preferred_element_type=jnp.float32)
    grad_packed = jnp.concatenate(
        [
            grad_queries.reshape(slot_count, head_span),
            grad_keys.reshape(slot_count, head_span),
            grad_values.reshape(slot_count, head_span),
        ],
        axis=1,
    ).astype(jnp.bfloat16)
    grad_hidden = lax.dot_general(
        grad_packed, w_qkv, (((1,), (1,)), ((), ())), preferred_element_type=jnp.float32
    )
    grad_normed = grad_hidden * gain_row
    grad_ln = inv_std * (
        grad_normed
        - jnp.mean(grad_normed, axis=-1, keepdims=True)
        - normed * jnp.mean(grad_normed * normed, axis=-1, keepdims=True)
    )
    grad_in = (masked.astype(jnp.float32) + grad_ln).astype(jnp.bfloat16)
    return (grad_in, hidden, grad_packed, masked, attn_out)


def per_device(activations, cotangent, counts, arrival, norm_gain, qkv_weight, out_weight):
    sections = lax.axis_size("section")
    section_idx = lax.axis_index("section")
    micro_count = cotangent.shape[0]
    slot_count = cotangent.shape[1]
    width_model = cotangent.shape[2]
    inputs_all = activations[0]
    gain_row = norm_gain[0]
    w_qkv = qkv_weight[0]
    w_out = out_weight[0]
    packed_width = w_qkv.shape[1]
    head_width = w_out.shape[1]
    visible_all = counts[:, 0]
    delay_steps = sections - 1 - section_idx

    def active(operands):
        grad_in, hidden, grad_packed, masked, attn_out = backward_layer(
            *operands, gain_row, w_qkv, w_out
        )
        return (grad_in, cross(hidden, grad_packed), cross(masked, attn_out))

    def resting(operands):
        blank_rows = jnp.zeros((slot_count, width_model), jnp.bfloat16)
        return (
            blank_rows,
            jnp.zeros((width_model, packed_width), jnp.float32),
            jnp.zeros((width_model, head_width), jnp.float32),
        )

    stored = (
        jnp.zeros((width_model, packed_width), jnp.float32),
        jnp.zeros((width_model, head_width), jnp.float32),
    )

    def advance(moment, carry):
        incoming, store_now = carry
        position = moment - delay_steps
        valid = (position >= 0) & (position < micro_count)
        clipped = jnp.clip(position, 0, micro_count - 1)
        chosen = arrival[clipped]
        inputs = lax.dynamic_index_in_dim(inputs_all, chosen, 0, keepdims=False)
        visible = lax.dynamic_index_in_dim(visible_all, chosen, 0, keepdims=False)
        own_grad = lax.dynamic_index_in_dim(cotangent, clipped, 0, keepdims=False)
        grad_out = jnp.where(section_idx == sections - 1, own_grad, incoming)
        results = lax.cond(valid, active, resting, (inputs, grad_out, visible))
        store_next = (store_now[0] + results[1], store_now[1] + results[2])
        passed = shifted(results[0], "section", -1)
        return (passed, store_next)

    start_grad = jnp.zeros((slot_count, width_model), jnp.bfloat16)
    leftover, store_final = lax.fori_loop(
        0, micro_count + sections - 1, advance, (start_grad, stored)
    )
    qkv_share, out_share = tuple(
        (
            part.astype(jnp.float32)
            for part in in_one_piece(
                (store_final[0].astype(jnp.bfloat16), store_final[1].astype(jnp.bfloat16)),
                "dp",
                0,
                1,
            )
        )
    )
    return (qkv_share[None], out_share[None])


def solution(mesh):
    placed = (
        P("section", None, "dp", None),
        P(None, "dp", None),
        P(None, "dp"),
        P(),
        P("section", None),
        P("section", None, None),
        P("section", None, None),
    )
    return jax.shard_map(
        per_device,
        mesh=mesh,
        in_specs=placed,
        out_specs=(P("section", "dp", None), P("section", "dp", None)),
        check_vma=False,
    )
```

profile of v0, /device:TPU:1, one launch (start us, length us, event | category | flops | bytes accessed | tf_op | source)
XLA Modules:
  0.0 715.6 jit_solution(6324335957163263954)
XLA Ops:
  8.2 607.3 %while.20 = (s32[]{:T(128)}, bf16[256,1280]{1,0:T(8,128)(2,1)}, f32[1280,1920]{1,0:T(8,128)}, f32[1280,640]{1,0:T(8,128)}, s32[]{:T(128)}, /*index=5*/s32[4]{0:T...) while((s32[]{:T(128)}, bf16[256,1280]{1,0:T(8,128)(2,1)}, ...), condition=%wide.region_10.11_spmd.clone, body=%wide.region_0.10_spmd.clone.sunk | while | flops 5153821696 | bytes 158626416 | solution.py:145
  15.0 8.6 %select_add_fusion.4 = f32[1280,1920]{1,0:T(8,128)} fusion(f32[1280,1920]{1,0:T(8,128)} %get-tuple-element.618, f32[1280,1920]{1,0:T(8,128)} %get-tuple-element.644, pred[]{:T(512)S(6)} %compare.3), kind=kLoop, calls=%fused_computation.58.clone.1 | loop fusion | flops 4915200 | bytes 29491200 | tf_op jit(solution)/shard_map/while/body/eval_jaxpr/add | solution.py:140
  25.6 7.2 %collective-permute-done = bf16[256,1280]{1,0:T(8,128)(2,1)} collective-permute-done((bf16[256,1280]{1,0:T(8,128)(2,1)}, bf16[256,1280]{1,0:T(8,128)(2,1)}, u32[]{:S(2)}, u32[]{:S(2)}) %collective-permute-start) | collective-permute-done | bytes 655392 | tf_op jit(solution)/shard_map/while/body/eval_jaxpr/ppermute | solution.py:16
  39.6 11.4 %select_add_fusion.4 = f32[1280,1920]{1,0:T(8,128)} fusion(f32[1280,1920]{1,0:T(8,128)} %get-tuple-element.618, f32[1280,1920]{1,0:T(8,128)} %get-tuple-element.644, pred[]{:T(512)S(6)} %compare.3), kind=kLoop, calls=%fused_computation.58.clone.1 | loop fusion | flops 4915200 | bytes 29491200 | tf_op jit(solution)/shard_map/while/body/eval_jaxpr/add | solution.py:140
  62.6 11.4 %select_add_fusion.4 = f32[1280,1920]{1,0:T(8,128)} fusion(f32[1280,1920]{1,0:T(8,128)} %get-tuple-element.618, f32[1280,1920]{1,0:T(8,128)} %get-tuple-element.644, pred[]{:T(512)S(6)} %compare.3), kind=kLoop, calls=%fused_computation.58.clone.1 | loop fusion | flops 4915200 | bytes 29491200 | tf_op jit(solution)/shard_map/while/body/eval_jaxpr/add | solution.py:140
  77.9 5.5 conditional.3
  84.8 11.4 %select_add_fusion.4 = f32[1280,1920]{1,0:T(8,128)} fusion(f32[1280,1920]{1,0:T(8,128)} %get-tuple-element.618, f32[1280,1920]{1,0:T(8,128)} %get-tuple-element.644, pred[]{:T(512)S(6)} %compare.3), kind=kLoop, calls=%fused_computation.58.clone.1 | loop fusion | flops 4915200 | bytes 29491200 | tf_op jit(solution)/shard_map/while/body/eval_jaxpr/add | solution.py:140
  109.6 11.4 %select_add_fusion.4 = f32[1280,1920]{1,0:T(8,128)} fusion(f32[1280,1920]{1,0:T(8,128)} %get-tuple-element.618, f32[1280,1920]{1,0:T(8,128)} %get-tuple-element.644, pred[]{:T(512)S(6)} %compare.3), kind=kLoop, calls=%fused_computation.58.clone.1 | loop fusion | flops 4915200 | bytes 29491200 | tf_op jit(solution)/shard_map/while/body/eval_jaxpr/add | solution.py:140
  133.2 11.4 %select_add_fusion.4 = f32[1280,1920]{1,0:T(8,128)} fusion(f32[1280,1920]{1,0:T(8,128)} %get-tuple-element.618, f32[1280,1920]{1,0:T(8,128)} %get-tuple-element.644, pred[]{:T(512)S(6)} %compare.3), kind=kLoop, calls=%fused_computation.58.clone.1 | loop fusion | flops 4915200 | bytes 29491200 | tf_op jit(solution)/shard_map/while/body/eval_jaxpr/add | solution.py:140
  155.8 11.4 %select_add_fusion.4 = f32[1280,1920]{1,0:T(8,128)} fusion(f32[1280,1920]{1,0:T(8,128)} %get-tuple-element.618, f32[1280,1920]{1,0:T(8,128)} %get-tuple-element.644, pred[]{:T(512)S(6)} %compare.3), kind=kLoop, calls=%fused_computation.58.clone.1 | loop fusion | flops 4915200 | bytes 29491200 | tf_op jit(solution)/shard_map/while/body/eval_jaxpr/add | solution.py:140
  171.2 222.2 %collective-permute-done = bf16[256,1280]{1,0:T(8,128)(2,1)} collective-permute-done((bf16[256,1280]{1,0:T(8,128)(2,1)}, bf16[256,1280]{1,0:T(8,128)(2,1)}, u32[]{:S(2)}, u32[]{:S(2)}) %collective-permute-start) | collective-permute-done | bytes 655392 | tf_op jit(solution)/shard_map/while/body/eval_jaxpr/ppermute | solution.py:16
  393.4 38.6 %conditional.3 = (bf16[256,1280]{1,0:T(8,128)(2,1)}, f32[1280,1920]{1,0:T(8,128)}, f32[1280,640]{1,0:T(8,128)S(1)}) conditional(s32[]{:T(128)} %convert_element_type.149, () %tuple.74, (s32[]{:T(128)}, s32[4]{0:T(128)}, s32[4]{0:T(128)}, pred[]{:T(512)}, bf16[4,256,1280]{2,1,0:T(8,128)(2,1)}, /*index=5*/bf16[256,1280]{1,0:T(8,128)(2,1)}, ...), branch_computations={%region_1.1_spmd, %region_2.9_spmd} | conditional | flops 5147268096 | bytes 116683056 | solution.py:139
  421.0 5.6 fusion.39
  433.3 11.4 %select_add_fusion.4 = f32[1280,1920]{1,0:T(8,128)} fusion(f32[1280,1920]{1,0:T(8,128)} %get-tuple-element.618, f32[1280,1920]{1,0:T(8,128)} %get-tuple-element.644, pred[]{:T(512)S(6)} %compare.3), kind=kLoop, calls=%fused_computation.58.clone.1 | loop fusion | flops 4915200 | bytes 29491200 | tf_op jit(solution)/shard_map/while/body/eval_jaxpr/add | solution.py:140
  448.7 38.6 %conditional.3 = (bf16[256,1280]{1,0:T(8,128)(2,1)}, f32[1280,1920]{1,0:T(8,128)}, f32[1280,640]{1,0:T(8,128)S(1)}) conditional(s32[]{:T(128)} %convert_element_type.149, () %tuple.74, (s32[]{:T(128)}, s32[4]{0:T(128)}, s32[4]{0:T(128)}, pred[]{:T(512)}, bf16[4,256,1280]{2,1,0:T(8,128)(2,1)}, /*index=5*/bf16[256,1280]{1,0:T(8,128)(2,1)}, ...), branch_computations={%region_1.1_spmd, %region_2.9_spmd} | conditional | flops 5147268096 | bytes 116683056 | solution.py:139
  476.3 5.6 fusion.39
  488.6 11.4 %select_add_fusion.4 = f32[1280,1920]{1,0:T(8,128)} fusion(f32[1280,1920]{1,0:T(8,128)} %get-tuple-element.618, f32[1280,1920]{1,0:T(8,128)} %get-tuple-element.644, pred[]{:T(512)S(6)} %compare.3), kind=kLoop, calls=%fused_computation.58.clone.1 | loop fusion | flops 4915200 | bytes 29491200 | tf_op jit(solution)/shard_map/while/body/eval_jaxpr/add | solution.py:140
  504.3 38.6 %conditional.3 = (bf16[256,1280]{1,0:T(8,128)(2,1)}, f32[1280,1920]{1,0:T(8,128)}, f32[1280,640]{1,0:T(8,128)S(1)}) conditional(s32[]{:T(128)} %convert_element_type.149, () %tuple.74, (s32[]{:T(128)}, s32[4]{0:T(128)}, s32[4]{0:T(128)}, pred[]{:T(512)}, bf16[4,256,1280]{2,1,0:T(8,128)(2,1)}, /*index=5*/bf16[256,1280]{1,0:T(8,128)(2,1)}, ...), branch_computations={%region_1.1_spmd, %region_2.9_spmd} | conditional | flops 5147268096 | bytes 116683056 | solution.py:139
  532.0 5.6 fusion.39
  544.2 11.4 %select_add_fusion.4 = f32[1280,1920]{1,0:T(8,128)} fusion(f32[1280,1920]{1,0:T(8,128)} %get-tuple-element.618, f32[1280,1920]{1,0:T(8,128)} %get-tuple-element.644, pred[]{:T(512)S(6)} %compare.3), kind=kLoop, calls=%fused_computation.58.clone.1 | loop fusion | flops 4915200 | bytes 29491200 | tf_op jit(solution)/shard_map/while/body/eval_jaxpr/add | solution.py:140
  560.2 38.6 %conditional.3 = (bf16[256,1280]{1,0:T(8,128)(2,1)}, f32[1280,1920]{1,0:T(8,128)}, f32[1280,640]{1,0:T(8,128)S(1)}) conditional(s32[]{:T(128)} %convert_element_type.149, () %tuple.74, (s32[]{:T(128)}, s32[4]{0:T(128)}, s32[4]{0:T(128)}, pred[]{:T(512)}, bf16[4,256,1280]{2,1,0:T(8,128)(2,1)}, /*index=5*/bf16[256,1280]{1,0:T(8,128)(2,1)}, ...), branch_computations={%region_1.1_spmd, %region_2.9_spmd} | conditional | flops 5147268096 | bytes 116683056 | solution.py:139
  587.9 5.6 fusion.39
  600.1 11.4 %select_add_fusion.4 = f32[1280,1920]{1,0:T(8,128)} fusion(f32[1280,1920]{1,0:T(8,128)} %get-tuple-element.618, f32[1280,1920]{1,0:T(8,128)} %get-tuple-element.644, pred[]{:T(512)S(6)} %compare.3), kind=kLoop, calls=%fused_computation.58.clone.1 | loop fusion | flops 4915200 | bytes 29491200 | tf_op jit(solution)/shard_map/while/body/eval_jaxpr/add | solution.py:140
  623.7 81.6 %reduce-scatter.2.cloned.1.call-done = bf16[80,2560]{1,0:T(8,128)(2,1)} async-done(((bf16[1280,2560]{1,0:T(8,128)(2,1)}), bf16[80,2560]{1,0:T(8,128)(2,1)}) %reduce-scatter.2.cloned.1.call-update) | async-done | bytes 409616 | tf_op jit(solution)/shard_map/reduce_scatter | solution.py:26
  (282 shorter events, 270.5 us)
Async XLA Ops:
  7.2 698.2 %reduce-scatter.2.cloned.1.call-start = ((), (), s32[]{:S(2)}) async-start(), calls=%async_computation.1 | async-start | bytes 6963200 | tf_op jit(solution)/shard_map/reduce_scatter | solution.py:26
  13.7 19.1 %collective-permute-start = (bf16[256,1280]{1,0:T(8,128)(2,1)}, bf16[256,1280]{1,0:T(8,128)(2,1)}, u32[]{:S(2)}, u32[]{:S(2)}) collective-permute-start(bf16[256,1280]{1,0:T(8,128)(2,1)} %get-tuple-element.617), channel_id=1, source_target_pairs={{16,0},{32,16},{48,32},{64,48},{80,64},{96,80},{112,96},{17,1},{33... | collective-permute-start | bytes 1966088 | tf_op jit(solution)/shard_map/while/body/eval_jaxpr/ppermute | solution.py:16
  38.3 17.4 %collective-permute-start = (bf16[256,1280]{1,0:T(8,128)(2,1)}, bf16[256,1280]{1,0:T(8,128)(2,1)}, u32[]{:S(2)}, u32[]{:S(2)}) collective-permute-start(bf16[256,1280]{1,0:T(8,128)(2,1)} %get-tuple-element.617), channel_id=1, source_target_pairs={{16,0},{32,16},{48,32},{64,48},{80,64},{96,80},{112,96},{17,1},{33... | collective-permute-start | bytes 1966088 | tf_op jit(solution)/shard_map/while/body/eval_jaxpr/ppermute | solution.py:16
  61.3 16.7 %collective-permute-start = (bf16[256,1280]{1,0:T(8,128)(2,1)}, bf16[256,1280]{1,0:T(8,128)(2,1)}, u32[]{:S(2)}, u32[]{:S(2)}) collective-permute-start(bf16[256,1280]{1,0:T(8,128)(2,1)} %get-tuple-element.617), channel_id=1, source_target_pairs={{16,0},{32,16},{48,32},{64,48},{80,64},{96,80},{112,96},{17,1},{33... | collective-permute-start | bytes 1966088 | tf_op jit(solution)/shard_map/while/body/eval_jaxpr/ppermute | solution.py:16
  83.5 19.3 %collective-permute-start = (bf16[256,1280]{1,0:T(8,128)(2,1)}, bf16[256,1280]{1,0:T(8,128)(2,1)}, u32[]{:S(2)}, u32[]{:S(2)}) collective-permute-start(bf16[256,1280]{1,0:T(8,128)(2,1)} %get-tuple-element.617), channel_id=1, source_target_pairs={{16,0},{32,16},{48,32},{64,48},{80,64},{96,80},{112,96},{17,1},{33... | collective-permute-start | bytes 1966088 | tf_op jit(solution)/shard_map/while/body/eval_jaxpr/ppermute | solution.py:16
  108.3 18.0 %collective-permute-start = (bf16[256,1280]{1,0:T(8,128)(2,1)}, bf16[256,1280]{1,0:T(8,128)(2,1)}, u32[]{:S(2)}, u32[]{:S(2)}) collective-permute-start(bf16[256,1280]{1,0:T(8,128)(2,1)} %get-tuple-element.617), channel_id=1, source_target_pairs={{16,0},{32,16},{48,32},{64,48},{80,64},{96,80},{112,96},{17,1},{33... | collective-permute-start | bytes 1966088 | tf_op jit(solution)/shard_map/while/body/eval_jaxpr/ppermute | solution.py:16
  131.9 17.2 %collective-permute-start = (bf16[256,1280]{1,0:T(8,128)(2,1)}, bf16[256,1280]{1,0:T(8,128)(2,1)}, u32[]{:S(2)}, u32[]{:S(2)}) collective-permute-start(bf16[256,1280]{1,0:T(8,128)(2,1)} %get-tuple-element.617), channel_id=1, source_target_pairs={{16,0},{32,16},{48,32},{64,48},{80,64},{96,80},{112,96},{17,1},{33... | collective-permute-start | bytes 1966088 | tf_op jit(solution)/shard_map/while/body/eval_jaxpr/ppermute | solution.py:16
  154.6 238.8 %collective-permute-start = (bf16[256,1280]{1,0:T(8,128)(2,1)}, bf16[256,1280]{1,0:T(8,128)(2,1)}, u32[]{:S(2)}, u32[]{:S(2)}) collective-permute-start(bf16[256,1280]{1,0:T(8,128)(2,1)} %get-tuple-element.617), channel_id=1, source_target_pairs={{16,0},{32,16},{48,32},{64,48},{80,64},{96,80},{112,96},{17,1},{33... | collective-permute-start | bytes 1966088 | tf_op jit(solution)/shard_map/while/body/eval_jaxpr/ppermute | solution.py:16
  415.3 5.4 copy-start.4
  421.0 5.6 copy-start.11
  421.0 7.4 %slice-start = ((s8[4915200]{0:T(1024)(128)(4,1)}), s8[4194304]{0:T(1024)(128)(4,1)S(1)}, s32[]{:S(2)}) async-start(s8[4915200]{0:T(1024)(128)(4,1)} %bitcast.97), calls=%async_computation.2 | async-start | bytes 8388608 | tf_op jit(solution)/shard_map/while/body/eval_jaxpr/cond
  432.0 16.7 %collective-permute-start = (bf16[256,1280]{1,0:T(8,128)(2,1)}, bf16[256,1280]{1,0:T(8,128)(2,1)}, u32[]{:S(2)}, u32[]{:S(2)}) collective-permute-start(bf16[256,1280]{1,0:T(8,128)(2,1)} %get-tuple-element.617), channel_id=1, source_target_pairs={{16,0},{32,16},{48,32},{64,48},{80,64},{96,80},{112,96},{17,1},{33... | collective-permute-start | bytes 1966088 | tf_op jit(solution)/shard_map/while/body/eval_jaxpr/ppermute | solution.py:16
  470.6 5.4 copy-start.4
  476.3 5.6 copy-start.11
  476.3 7.4 %slice-start = ((s8[4915200]{0:T(1024)(128)(4,1)}), s8[4194304]{0:T(1024)(128)(4,1)S(1)}, s32[]{:S(2)}) async-start(s8[4915200]{0:T(1024)(128)(4,1)} %bitcast.97), calls=%async_computation.2 | async-start | bytes 8388608 | tf_op jit(solution)/shard_map/while/body/eval_jaxpr/cond
  487.3 17.1 %collective-permute-start = (bf16[256,1280]{1,0:T(8,128)(2,1)}, bf16[256,1280]{1,0:T(8,128)(2,1)}, u32[]{:S(2)}, u32[]{:S(2)}) collective-permute-start(bf16[256,1280]{1,0:T(8,128)(2,1)} %get-tuple-element.617), channel_id=1, source_target_pairs={{16,0},{32,16},{48,32},{64,48},{80,64},{96,80},{112,96},{17,1},{33... | collective-permute-start | bytes 1966088 | tf_op jit(solution)/shard_map/while/body/eval_jaxpr/ppermute | solution.py:16
  526.3 5.4 copy-start.4
  532.0 5.6 copy-start.11
  532.0 7.4 %slice-start = ((s8[4915200]{0:T(1024)(128)(4,1)}), s8[4194304]{0:T(1024)(128)(4,1)S(1)}, s32[]{:S(2)}) async-start(s8[4915200]{0:T(1024)(128)(4,1)} %bitcast.97), calls=%async_computation.2 | async-start | bytes 8388608 | tf_op jit(solution)/shard_map/while/body/eval_jaxpr/cond
  542.9 17.3 %collective-permute-start = (bf16[256,1280]{1,0:T(8,128)(2,1)}, bf16[256,1280]{1,0:T(8,128)(2,1)}, u32[]{:S(2)}, u32[]{:S(2)}) collective-permute-start(bf16[256,1280]{1,0:T(8,128)(2,1)} %get-tuple-element.617), channel_id=1, source_target_pairs={{16,0},{32,16},{48,32},{64,48},{80,64},{96,80},{112,96},{17,1},{33... | collective-permute-start | bytes 1966088 | tf_op jit(solution)/shard_map/while/body/eval_jaxpr/ppermute | solution.py:16
  582.2 5.4 copy-start.4
  587.9 5.6 copy-start.11
  587.9 7.4 %slice-start = ((s8[4915200]{0:T(1024)(128)(4,1)}), s8[4194304]{0:T(1024)(128)(4,1)S(1)}, s32[]{:S(2)}) async-start(s8[4915200]{0:T(1024)(128)(4,1)} %bitcast.97), calls=%async_computation.2 | async-start | bytes 8388608 | tf_op jit(solution)/shard_map/while/body/eval_jaxpr/cond
  598.8 16.7 %collective-permute-start = (bf16[256,1280]{1,0:T(8,128)(2,1)}, bf16[256,1280]{1,0:T(8,128)(2,1)}, u32[]{:S(2)}, u32[]{:S(2)}) collective-permute-start(bf16[256,1280]{1,0:T(8,128)(2,1)} %get-tuple-element.617), channel_id=1, source_target_pairs={{16,0},{32,16},{48,32},{64,48},{80,64},{96,80},{112,96},{17,1},{33... | collective-permute-start | bytes 1966088 | tf_op jit(solution)/shard_map/while/body/eval_jaxpr/ppermute | solution.py:16
  (41 other events, 76.0 us)
Sparse Core Ops, SparseCore 0:
  623.8 81.4 reduce-scatter.1
where the time goes:
time: 719 us; the launch traced here: 716 us
  waiting for transfers between devices  317 us (44%)
  other arithmetic  203 us (28%)
  matrix products  97.2 us (14%)
  local copies, waits for them, and re-layouts  60.7 us (8%)
  starting transfers between devices  14.1 us (2%)
  between operations  14.1 us (2%)
  loops' own time  8.74 us (1%)
    ppermute x11, waiting for transfers between devices, shifted(): lax.ppermute(value, axis, [(source, source + steps) for source in range(i...  236 us
    add x22, other arithmetic, advance(): store_next = (store_now[0] + results[1], store_now[1] + results[2])  164 us
    reduce_scatter x1, waiting for transfers between devices, in_one_piece(): lax.psum_scatter(both, axis, scatter_dimension=dim, tiled=True)  81.6 us
    another operation x22, local copies, waits for them, and re-layouts  39.6 us
    dot_general x8, matrix products, cross(): lax.dot_general(left, right, (((0,), (0,)), ((), ())), preferred_element_...  25.1 us
    dot_general x4, matrix products, backward_layer(): jnp.dot(hidden, w_qkv, preferred_element_type=jnp.float32)  17 us
  transfers between devices with their start and end apart: 12, of which 9 were waited for; matrix products, arithmetic and copies ran while one was open for 23% of the time, Pallas kernels for 0%

commit v1 on v0

v1 whole, which is shorter than its diff:
```python
import functools

import jax
import jax.numpy as jnp
from jax import lax
from jax.experimental import pallas as pl
from jax.experimental.pallas import tpu as pltpu
from jax.sharding import PartitionSpec as P

HDIM = 80
HEADS = 8
EPSILON = 1e-06
MESH = pl.DeviceIdType.MESH
F32 = jnp.float32
BF16 = jnp.bfloat16


def dot_nn(a, b):
    return lax.dot_general(a, b, (((1,), (0,)), ((), ())), preferred_element_type=F32)


def dot_nt(a, b):
    return lax.dot_general(a, b, (((1,), (1,)), ((), ())), preferred_element_type=F32)


def loop(count, body):
    def step(i, carry):
        body(i)
        return carry

    lax.fori_loop(0, count, step, 0)


def rows_at(i, size):
    return pl.ds(pl.multiple_of(i * size, size), size)


def pipeline_kernel(
    sections,
    counts_ref,
    arrival_ref,
    x_ref,
    cot_ref,
    gain_ref,
    wqkv_ref,
    wo_ref,
    out_ref,
    wqkv_t,
    wo_t,
    gain_b,
    x_t,
    norm_t,
    hid_t,
    stats,
    pk_t,
    v_n,
    prob_f,
    prob_h,
    attn_t,
    ga_t,
    gpk_t,
    gn_t,
    acc_q,
    acc_o,
    g_recv,
    g_send,
    send_sem,
    recv_sem,
):
    micro, slots, width = x_ref.shape
    head_span = wo_ref.shape[1]
    packed = wqkv_ref.shape[1]
    scale = HDIM**-0.5
    sec = lax.axis_index("section")
    below = lax.rem(sec + sections - 1, sections)
    above = lax.rem(sec + 1, sections)
    barrier = pltpu.get_barrier_semaphore()
    for other in (below, above):
        pl.semaphore_signal(barrier, inc=1, device_id={"section": other}, device_id_type=MESH)
    pl.semaphore_wait(barrier, 2)

    def turn_wo(c):
        wo_t[:, rows_at(c, 256)] = wo_ref[rows_at(c, 256), :].T

    def turn_wqkv(c):
        wqkv_t[:, rows_at(c, 256)] = wqkv_ref[rows_at(c, 256), :].T

    loop(width // 256, turn_wqkv)
    loop(width // 256, turn_wo)
    gain_b[...] = jnp.broadcast_to(gain_ref[...], (128, width)).T

    CH = 160
    chunks = width // CH

    def gain_rows(c, size):
        part = gain_b[rows_at(c, size), :]
        return jnp.concatenate([part] * (slots // 128), axis=1)

    def forward(p):
        chosen = arrival_ref[p]
        count = counts_ref[chosen]

        def turn(c):
            x_t[rows_at(c, 256), :] = x_ref[chosen, :, rows_at(c, 256)].T

        loop(width // 256, turn)

        def add(c, total):
            return total + jnp.sum(x_t[rows_at(c, CH), :].astype(F32), axis=0, keepdims=True)

        zero = jnp.zeros((1, slots), F32)
        mean = lax.fori_loop(0, chunks, add, zero) * (1.0 / width)

        def add_sq(c, total):
            centered = x_t[rows_at(c, CH), :].astype(F32) - mean
            return total + jnp.sum(centered * centered, axis=0, keepdims=True)

        var = lax.fori_loop(0, chunks, add_sq, zero) * (1.0 / width)
        inv = lax.rsqrt(var + EPSILON)
        stats[0:1, :] = inv

        def norm(c):
            normed = (x_t[rows_at(c, CH), :].astype(F32) - mean) * inv
            norm_t[rows_at(c, CH), :] = normed
            hid_t[rows_at(c, CH), :] = (normed * gain_rows(c, CH)).astype(BF16)

        loop(chunks, norm)

        def pack(m):
            pk_t[rows_at(m, 480), :] = dot_nn(wqkv_t[rows_at(m, 480), :], hid_t[...]).astype(BF16)

        loop(packed // 480, pack)
        keep = lax.broadcasted_iota(jnp.int32, (slots, slots), 0) < count

        def head(h):
            q = pk_t[rows_at(h, HDIM), :]
            k = pk_t[rows_at(h + HEADS, HDIM), :]
            v = pk_t[rows_at(h + 2 * HEADS, HDIM), :]
            s = dot_nn(k.T, q) * scale
            s = jnp.where(keep, s, -1e30)
            e = jnp.exp(s - jnp.max(s, axis=0, keepdims=True))
            prob = e * (1.0 / jnp.sum(e, axis=0, keepdims=True))
            prob_f[h] = prob
            half = prob.astype(BF16)
            prob_h[h] = half
            v_n[h] = v.T
            attn_t[rows_at(h, HDIM), :] = dot_nn(v, half).astype(BF16)

        loop(HEADS, head)

    def take_cotangent(p):
        count = counts_ref[arrival_ref[p]]
        keep = (lax.broadcasted_iota(jnp.int32, (1, slots), 1) < count).astype(F32)

        def turn(c):
            piece = cot_ref[p, :, rows_at(c, 256)].T.astype(F32) * keep
            g_recv[p, rows_at(c, 256), :] = piece.astype(BF16)

        loop(width // 256, turn)

    def hop(p):
        return pltpu.make_async_remote_copy(
            src_ref=g_send.at[p],
            dst_ref=g_recv.at[p],
            send_sem=send_sem.at[p],
            recv_sem=recv_sem.at[p],
            device_id={"section": below},
            device_id_type=MESH,
        )

    def backward(p):
        def grad_attn(m):
            ga_t[rows_at(m, 320), :] = dot_nn(wo_t[rows_at(m, 320), :], g_recv[p]).astype(BF16)

        loop(head_span // 320, grad_attn)

        def head(h):
            q = pk_t[rows_at(h, HDIM), :]
            k = pk_t[rows_at(h + HEADS, HDIM), :]
            ga = ga_t[rows_at(h, HDIM), :]
            prob = prob_f[h]
            grad_prob = dot_nn(v_n[h], ga)
            inner = jnp.sum(prob * grad_prob, axis=0, keepdims=True)
            gs = (prob * (grad_prob - inner) * scale).astype(BF16)
            gpk_t[rows_at(h, HDIM), :] = dot_nn(k, gs).astype(BF16)
            gpk_t[rows_at(h + HEADS, HDIM), :] = dot_nt(q, gs).astype(BF16)
            gpk_t[rows_at(h + 2 * HEADS, HDIM), :] = dot_nt(ga, prob_h[h]).astype(BF16)

        loop(HEADS, head)

    def pass_down(p):
        def grad_hidden(m, sums):
            gn = dot_nn(wqkv_ref[rows_at(m, 320), :], gpk_t[...]) * gain_rows(m, 320)
            gn_t[rows_at(m, 320), :] = gn
            return (
                sums[0] + jnp.sum(gn, axis=0, keepdims=True),
                sums[1] + jnp.sum(gn * norm_t[rows_at(m, 320), :], axis=0, keepdims=True),
            )

        zero = jnp.zeros((1, slots), F32)
        first, second = lax.fori_loop(0, width // 320, grad_hidden, (zero, zero))
        first = first * (1.0 / width)
        second = second * (1.0 / width)
        inv = stats[0:1, :]

        def finish(c):
            at = rows_at(c, CH)
            grad_ln = inv * (gn_t[at, :] - first - norm_t[at, :] * second)
            g_send[p, at, :] = (g_recv[p, at, :].astype(F32) + grad_ln).astype(BF16)

        loop(chunks, finish)
        hop(p).start()

    def weights(p):
        def qkv(n):
            acc_q[:, rows_at(n, 256)] += dot_nt(hid_t[...], gpk_t[rows_at(n, 256), :])

        loop(packed // 256, qkv)
        tail = packed // 256 * 256
        acc_q[:, tail:packed] += dot_nt(hid_t[...], gpk_t[tail:packed, :])

        def out(n):
            acc_o[:, rows_at(n, 256)] += dot_nt(g_recv[p], attn_t[rows_at(n, 256), :])

        loop(head_span // 256, out)
        tail = head_span // 256 * 256
        acc_o[:, tail:head_span] += dot_nt(g_recv[p], attn_t[tail:head_span, :])

    def clear(c):
        acc_q[rows_at(c, 64), :] = jnp.zeros((64, packed), F32)
        acc_o[rows_at(c, 64), :] = jnp.zeros((64, head_span), F32)

    forward(0)

    def moment(p):
        @pl.when(sec == sections - 1)
        def _():
            take_cotangent(p)

        @pl.when(sec < sections - 1)
        def _():
            hop(p).wait_recv()

        backward(p)

        @pl.when(sec > 0)
        def _():
            pass_down(p)

        @pl.when(p == 0)
        def _():
            loop(width // 64, clear)

        weights(p)

        @pl.when(p < micro - 1)
        def _():
            forward(p + 1)

    loop(micro, moment)

    @pl.when(sec > 0)
    def _():
        def drain(p):
            hop(p).wait_send()

        loop(micro, drain)

    def finish(c):
        out_ref[rows_at(c, 64), 0:packed] = acc_q[rows_at(c, 64), :].astype(BF16)
        out_ref[rows_at(c, 64), packed:] = acc_o[rows_at(c, 64), :].astype(BF16)

    loop(width // 64, finish)


def run_pipeline(sections, counts, arrival, x, cotangent, gain, wqkv, wo):
    micro, slots, width = x.shape
    packed, head_span = wqkv.shape[1], wo.shape[1]
    vmem = pl.BlockSpec(memory_space=pltpu.VMEM)
    smem = pl.BlockSpec(memory_space=pltpu.SMEM)
    scratch = [
        pltpu.VMEM((packed, width), BF16),
        pltpu.VMEM((head_span, width), BF16),
        pltpu.VMEM((width, 128), F32),
        pltpu.VMEM((width, slots), BF16),
        pltpu.VMEM((width, slots), F32),
        pltpu.VMEM((width, slots), BF16),
        pltpu.VMEM((8, slots), F32),
        pltpu.VMEM((packed, slots), BF16),
        pltpu.VMEM((HEADS, slots, HDIM), BF16),
        pltpu.VMEM((HEADS, slots, slots), F32),
        pltpu.VMEM((HEADS, slots, slots), BF16),
        pltpu.VMEM((head_span, slots), BF16),
        pltpu.VMEM((head_span, slots), BF16),
        pltpu.VMEM((packed, slots), BF16),
        pltpu.VMEM((width, slots), F32),
        pltpu.VMEM((width, packed), F32),
        pltpu.VMEM((width, head_span), F32),
        pltpu.VMEM((micro, width, slots), BF16),
        pltpu.VMEM((micro, width, slots), BF16),
        pltpu.SemaphoreType.DMA((micro,)),
        pltpu.SemaphoreType.DMA((micro,)),
    ]
    return pl.pallas_call(
        functools.partial(pipeline_kernel, sections),
        out_shape=jax.ShapeDtypeStruct((width, packed + head_span), BF16),
        in_specs=[smem, smem, vmem, vmem, vmem, vmem, vmem],
        out_specs=vmem,
        scratch_shapes=scratch,
        compiler_params=pltpu.CompilerParams(
            collective_id=0, has_side_effects=True, vmem_limit_bytes=64 * 1024 * 1024 - 65536
        ),
        name="pipeline",
    )(counts, arrival, x, cotangent, gain, wqkv, wo)


def per_device(activations, cotangent, counts, arrival, norm_gain, qkv_weight, out_weight):
    sections = lax.axis_size("section")
    packed = qkv_weight.shape[2]
    both = run_pipeline(
        sections,
        counts[:, 0],
        arrival,
        activations[0],
        cotangent,
        norm_gain,
        qkv_weight[0],
        out_weight[0],
    )
    share = lax.psum_scatter(both, "dp", scatter_dimension=0, tiled=True).astype(F32)
    return (share[None, :, :packed], share[None, :, packed:])


def solution(mesh):
    placed = (
        P("section", None, "dp", None),
        P(None, "dp", None),
        P(None, "dp"),
        P(),
        P("section", None),
        P("section", None, None),
        P("section", None, None),
    )
    return jax.shard_map(
        per_device,
        mesh=mesh,
        in_specs=placed,
        out_specs=(P("section", "dp", None), P("section", "dp", None)),
        check_vma=False,
    )
```

time: 719 us -> 329 us (0.46)
  waiting for transfers between devices: 317 us -> 79.6 us
  Pallas kernels: 0 us -> 232 us
  other arithmetic: 203 us -> 1.06 us
  matrix products: 97.2 us -> 0 us
  local copies, waits for them, and re-layouts: 60.7 us -> 1.56 us
  starting transfers between devices: 14.1 us -> 0.04 us
  loops' own time: 8.74 us -> 0 us
    ppermute x11 -> x0, waiting for transfers between devices: 236 us -> none  [shifted(): lax.ppermute(value, axis, [(source, source + steps) for source in range(i...]
    pallas_call x0 -> x1, Pallas kernels: none -> 232 us  [run_pipeline(): pl.pallas_call(functools.partial(pipeline_kernel, sections), out_shape=ja...]
    add x22 -> x0, other arithmetic: 164 us -> none  [advance(): store_next = (store_now[0] + results[1], store_now[1] + results[2])]
    dot_general x40 -> x0, matrix products: 88.5 us -> none  [the longest x8 25.1 us: cross(): lax.dot_general(left, right, (((0,), (0,)), ((), ())), preferred_element_...]
    another operation x22 -> x0, local copies, waits for them, and re-layouts: 39.6 us -> none
    ppermute x11 -> x0, starting transfers between devices: 14.1 us -> none  [shifted(): lax.ppermute(value, axis, [(source, source + steps) for source in range(i...]
    reduce_sum x8 -> x0, other arithmetic: 10.6 us -> none  [the longest x4 5.62 us: backward_layer(): jnp.mean(centered * centered, axis=-1, keepdims=True) + EPSILON]
    cond x104 -> x0, local copies, waits for them, and re-layouts: 10.1 us -> none
  transfers between devices with their start and end apart: 12 -> 1, of which waited for: 9 -> 1; matrix products, arithmetic and copies ran while one was open for 23% -> 0% of each run, Pallas kernels for 0% -> 0%
where the time goes in v1:
time: 329 us; the launch traced here: 328 us
  Pallas kernels  232 us (71%)
  waiting for transfers between devices  79.6 us (24%)
  between operations  14 us (4%)
    pallas_call x1, Pallas kernels, run_pipeline(): pl.pallas_call(functools.partial(pipeline_kernel, sections), out_shape=ja...  232 us
    reduce_scatter x1, waiting for transfers between devices, per_device(): lax.psum_scatter(both, 'dp', scatter_dimension=0, tiled=True).astype(F32)  79.6 us
  transfers between devices with their start and end apart: 1, of which 1 were waited for; matrix products, arithmetic and copies ran while one was open for 0% of the time, Pallas kernels for 0%

profile of v1, /device:TPU:1, one launch (start us, length us, event | category | flops | bytes accessed | tf_op | source)
XLA Modules:
  0.0 328.3 jit_solution(5448584062625528404)
XLA Ops:
  7.2 0.0 reduce-scatter.2.cloned.1.call-start
  7.2 232.0 %pipeline.1 = bf16[1280,2560]{1,0:T(8,128)(2,1)} custom-call(s32[4]{0:T(128)} %bitcast.11, s32[4]{0:T(128)} %arrival_ref.1, bf16[4,256,1280]{2,1,0:T(8,128)(2,1)} %bitcast.9, bf16[4,256,1280]{2,1,0:T(8,128)(2,1)} %cot_ref.1, f32[1,1280]{1,0:T(1,128)} %gain_ref.1, bf16[1280,1920]{1,0:T(8,128)(2,1)} %bitcast.8, bf16[1280,640]{1,0:T(8,128)(2,1)} %bitcast.10), custom_call_target="tpu_custom_call" | custom-call | tf_op jit(solution)/shard_map/pipeline/pallas_call | solution.py:304
  239.2 0.0 reduce-scatter.2.cloned.1.call-update
  239.2 79.6 %reduce-scatter.2.cloned.1.call-done = bf16[80,2560]{1,0:T(8,128)(2,1)} async-done(((bf16[1280,2560]{1,0:T(8,128)(2,1)}), bf16[80,2560]{1,0:T(8,128)(2,1)}) %reduce-scatter.2.cloned.1.call-update) | async-done | bytes 409616 | tf_op jit(solution)/shard_map/reduce_scatter | solution.py:330
  318.8 1.1 convert_element_type.3
  319.9 0.7 slice_bitcast_fusion.1
  320.6 0.9 slice_bitcast_fusion
Async XLA Ops:
  7.2 311.6 %reduce-scatter.2.cloned.1.call-start = ((), (), s32[]{:S(2)}) async-start(), calls=%async_computation.1 | async-start | bytes 6963200 | tf_op jit(solution)/shard_map/reduce_scatter | solution.py:330
Sparse Core Ops, SparseCore 0:
  239.3 79.4 reduce-scatter.1

commit v2 on v1

--- a/solution.py
+++ b/solution.py
@@ -23,6 +23,10 @@
     return lax.dot_general(a, b, (((1,), (1,)), ((), ())), preferred_element_type=F32)
 
 
+def fold(a):
+    return jnp.sum(a.reshape(a.shape[0] // 8, 8, a.shape[1]), axis=0)
+
+
 def loop(count, body):
     def step(i, carry):
         body(i)
@@ -32,6 +36,8 @@
 
 
 def rows_at(i, size):
+    if isinstance(i, int):
+        return pl.ds(i * size, size)
     return pl.ds(pl.multiple_of(i * size, size), size)
 
 
@@ -58,14 +64,16 @@
     prob_h,
     attn_t,
     ga_t,
+    ga_acc,
     gpk_t,
-    gn_t,
+    gain_w,
     acc_q,
     acc_o,
     g_recv,
     g_send,
     send_sem,
     recv_sem,
+    go_sem,
 ):
     micro, slots, width = x_ref.shape
     head_span = wo_ref.shape[1]
@@ -74,10 +82,14 @@
     sec = lax.axis_index("section")
     below = lax.rem(sec + sections - 1, sections)
     above = lax.rem(sec + 1, sections)
+    lane = lax.axis_index("dp")
+    core = lax.rem(lane, 2)
+    twin = lane + 1 - 2 * core
     barrier = pltpu.get_barrier_semaphore()
     for other in (below, above):
         pl.semaphore_signal(barrier, inc=1, device_id={"section": other}, device_id_type=MESH)
-    pl.semaphore_wait(barrier, 2)
+    pl.semaphore_signal(barrier, inc=1, device_id={"dp": twin}, device_id_type=MESH)
+    pl.semaphore_wait(barrier, 3)
 
     def turn_wo(c):
         wo_t[:, rows_at(c, 256)] = wo_ref[rows_at(c, 256), :].T
@@ -89,7 +101,17 @@
     loop(width // 256, turn_wo)
     gain_b[...] = jnp.broadcast_to(gain_ref[...], (128, width)).T
 
+    gain_hi = gain_b[...].astype(BF16)
+    gain_lo = (gain_b[...] - gain_hi.astype(F32)).astype(BF16)
+    gains = jnp.concatenate([gain_hi, gain_lo], axis=1)
+
+    def weigh(m):
+        both = dot_nn(wqkv_t[rows_at(m, 480), :], gains) * (1.0 / width)
+        gain_w[rows_at(m, 480), :] = both[:, :128] + both[:, 128:]
+
     CH = 160
+    PIECE = 256
+    pieces = width // PIECE
     chunks = width // CH
 
     def gain_rows(c, size):
@@ -100,22 +122,21 @@
         chosen = arrival_ref[p]
         count = counts_ref[chosen]
 
-        def turn(c):
-            x_t[rows_at(c, 256), :] = x_ref[chosen, :, rows_at(c, 256)].T
-
-        loop(width // 256, turn)
-
-        def add(c, total):
-            return total + jnp.sum(x_t[rows_at(c, CH), :].astype(F32), axis=0, keepdims=True)
-
-        zero = jnp.zeros((1, slots), F32)
-        mean = lax.fori_loop(0, chunks, add, zero) * (1.0 / width)
+        def turn(c, total):
+            piece = x_ref[chosen, :, rows_at(c, 256)].T
+            x_t[rows_at(c, 256), :] = piece
+            return total + fold(piece.astype(F32))
+
+        zero = jnp.zeros((8, slots), F32)
+        total = lax.fori_loop(0, width // 256, turn, zero)
+        mean = jnp.sum(total, axis=0, keepdims=True) * (1.0 / width)
 
         def add_sq(c, total):
-            centered = x_t[rows_at(c, CH), :].astype(F32) - mean
-            return total + jnp.sum(centered * centered, axis=0, keepdims=True)
-
-        var = lax.fori_loop(0, chunks, add_sq, zero) * (1.0 / width)
+            centered = x_t[rows_at(c, 320), :].astype(F32) - mean
+            return total + fold(centered * centered)
+
+        total = lax.fori_loop(0, width // 320, add_sq, zero)
+        var = jnp.sum(total, axis=0, keepdims=True) * (1.0 / width)
         inv = lax.rsqrt(var + EPSILON)
         stats[0:1, :] = inv
 
@@ -146,70 +167,80 @@
             v_n[h] = v.T
             attn_t[rows_at(h, HDIM), :] = dot_nn(v, half).astype(BF16)
 
-        loop(HEADS, head)
-
-    def take_cotangent(p):
+        for h in range(HEADS):
+            head(h)
+
+    def take_cotangent(p, c):
         count = counts_ref[arrival_ref[p]]
         keep = (lax.broadcasted_iota(jnp.int32, (1, slots), 1) < count).astype(F32)
-
-        def turn(c):
-            piece = cot_ref[p, :, rows_at(c, 256)].T.astype(F32) * keep
-            g_recv[p, rows_at(c, 256), :] = piece.astype(BF16)
-
-        loop(width // 256, turn)
-
-    def hop(p):
+        piece = cot_ref[p, :, rows_at(c, PIECE)].T.astype(F32) * keep
+        g_recv[p, rows_at(c, PIECE), :] = piece.astype(BF16)
+
+    def hop(p, c):
         return pltpu.make_async_remote_copy(
-            src_ref=g_send.at[p],
-            dst_ref=g_recv.at[p],
-            send_sem=send_sem.at[p],
-            recv_sem=recv_sem.at[p],
+            src_ref=g_send.at[p, rows_at(c, PIECE)],
+            dst_ref=g_recv.at[p, rows_at(c, PIECE)],
+            send_sem=send_sem.at[p, c],
+            recv_sem=recv_sem.at[p, c],
             device_id={"section": below},
             device_id_type=MESH,
         )
 
     def backward(p):
-        def grad_attn(m):
-            ga_t[rows_at(m, 320), :] = dot_nn(wo_t[rows_at(m, 320), :], g_recv[p]).astype(BF16)
-
-        loop(head_span // 320, grad_attn)
-
-        def head(h):
+        for c in range(pieces):
+
+            @pl.when(sec == sections - 1)
+            def _():
+                take_cotangent(p, c)
+
+            @pl.when(sec < sections - 1)
+            def _():
+                hop(p, c).wait_recv()
+
+            part = dot_nn(wo_t[:, rows_at(c, PIECE)], g_recv[p, rows_at(c, PIECE), :])
+            if c == 0:
+                ga_acc[...] = part
+            elif c < pieces - 1:
+                ga_acc[...] += part
+            else:
+                ga_t[...] = (ga_acc[...] + part).astype(BF16)
+
+        first = jnp.zeros((8, slots), F32)
+        second = jnp.zeros((8, slots), F32)
+        for h in range(HEADS):
             q = pk_t[rows_at(h, HDIM), :]
             k = pk_t[rows_at(h + HEADS, HDIM), :]
+            v = pk_t[rows_at(h + 2 * HEADS, HDIM), :]
             ga = ga_t[rows_at(h, HDIM), :]
             prob = prob_f[h]
             grad_prob = dot_nn(v_n[h], ga)
             inner = jnp.sum(prob * grad_prob, axis=0, keepdims=True)
             gs = (prob * (grad_prob - inner) * scale).astype(BF16)
-            gpk_t[rows_at(h, HDIM), :] = dot_nn(k, gs).astype(BF16)
-            gpk_t[rows_at(h + HEADS, HDIM), :] = dot_nt(q, gs).astype(BF16)
-            gpk_t[rows_at(h + 2 * HEADS, HDIM), :] = dot_nt(ga, prob_h[h]).astype(BF16)
-
-        loop(HEADS, head)
-
-    def pass_down(p):
-        def grad_hidden(m, sums):
-            gn = dot_nn(wqkv_ref[rows_at(m, 320), :], gpk_t[...]) * gain_rows(m, 320)
-            gn_t[rows_at(m, 320), :] = gn
-            return (
-                sums[0] + jnp.sum(gn, axis=0, keepdims=True),
-                sums[1] + jnp.sum(gn * norm_t[rows_at(m, 320), :], axis=0, keepdims=True),
-            )
-
-        zero = jnp.zeros((1, slots), F32)
-        first, second = lax.fori_loop(0, width // 320, grad_hidden, (zero, zero))
-        first = first * (1.0 / width)
-        second = second * (1.0 / width)
+            grads = (dot_nn(k, gs), dot_nt(q, gs), dot_nt(ga, prob_h[h]))
+            for i, (grad, own) in enumerate(zip(grads, (q, k, v))):
+                at = rows_at(h + i * HEADS, HDIM)
+                half = grad.astype(BF16)
+                gpk_t[at, :] = half
+                full = half.astype(F32)
+                w = gain_w[at, :]
+                first += fold(full * jnp.concatenate([w] * (slots // 128), axis=1))
+                second += fold(full * own.astype(F32))
+        return (
+            jnp.sum(first, axis=0, keepdims=True),
+            jnp.sum(second, axis=0, keepdims=True) * (1.0 / width),
+        )
+
+    def pass_down(p, first, second):
         inv = stats[0:1, :]
 
-        def finish(c):
-            at = rows_at(c, CH)
-            grad_ln = inv * (gn_t[at, :] - first - norm_t[at, :] * second)
+        def grad_hidden(c):
+            at = rows_at(c, PIECE)
+            gn = dot_nn(wqkv_ref[at, :], gpk_t[...]) * gain_rows(c, PIECE)
+            grad_ln = inv * (gn - first - norm_t[at, :] * second)
             g_send[p, at, :] = (g_recv[p, at, :].astype(F32) + grad_ln).astype(BF16)
-
-        loop(chunks, finish)
-        hop(p).start()
+            hop(p, c).start()
+
+        loop(pieces, grad_hidden)
 
     def weights(p):
         def qkv(n):
@@ -231,27 +262,28 @@
         acc_o[rows_at(c, 64), :] = jnp.zeros((64, head_span), F32)
 
     forward(0)
+    loop(packed // 480, weigh)
 
     def moment(p):
-        @pl.when(sec == sections - 1)
-        def _():
-            take_cotangent(p)
-
-        @pl.when(sec < sections - 1)
-        def _():
-            hop(p).wait_recv()
-
-        backward(p)
+        sums = backward(p)
+
+        @pl.when((sec == sections - 1) & (p == 0) & (core == 1))
+        def _():
+            pl.semaphore_wait(go_sem, 1)
 
         @pl.when(sec > 0)
         def _():
-            pass_down(p)
+            pass_down(p, *sums)
 
         @pl.when(p == 0)
         def _():
             loop(width // 64, clear)
 
         weights(p)
+
+        @pl.when((sec == sections - 1) & (p == 0) & (core == 0))
+        def _():
+            pl.semaphore_signal(go_sem, inc=1, device_id={"dp": twin}, device_id_type=MESH)
 
         @pl.when(p < micro - 1)
         def _():
@@ -262,7 +294,8 @@
     @pl.when(sec > 0)
     def _():
         def drain(p):
-            hop(p).wait_send()
+            for c in range(pieces):
+                hop(p, c).wait_send()
 
         loop(micro, drain)
 
@@ -292,14 +325,16 @@
         pltpu.VMEM((HEADS, slots, slots), BF16),
         pltpu.VMEM((head_span, slots), BF16),
         pltpu.VMEM((head_span, slots), BF16),
+        pltpu.VMEM((head_span, slots), F32),
         pltpu.VMEM((packed, slots), BF16),
-        pltpu.VMEM((width, slots), F32),
+        pltpu.VMEM((packed, 128), F32),
         pltpu.VMEM((width, packed), F32),
         pltpu.VMEM((width, head_span), F32),
         pltpu.VMEM((micro, width, slots), BF16),
         pltpu.VMEM((micro, width, slots), BF16),
-        pltpu.SemaphoreType.DMA((micro,)),
-        pltpu.SemaphoreType.DMA((micro,)),
+        pltpu.SemaphoreType.DMA((micro, width // 256)),
+        pltpu.SemaphoreType.DMA((micro, width // 256)),
+        pltpu.SemaphoreType.REGULAR,
     ]
     return pl.pallas_call(
         functools.partial(pipeline_kernel, sections),

time: 329 us -> 278 us (0.84)
  Pallas kernels: 232 us -> 186 us
  waiting for transfers between devices: 79.6 us -> 75.3 us
    pallas_call x1, Pallas kernels: 232 us -> 186 us  [run_pipeline(): pl.pallas_call(functools.partial(pipeline_kernel, sections), out_shape=ja...]
    reduce_scatter x1, waiting for transfers between devices: 79.6 us -> 75.3 us  [per_device(): lax.psum_scatter(both, 'dp', scatter_dimension=0, tiled=True).astype(F32)]
where the time goes in v2:
time: 278 us
  Pallas kernels  186 us (67%)
  waiting for transfers between devices  75.3 us (27%)
  between operations  14 us (5%)
    pallas_call x1, Pallas kernels, run_pipeline(): pl.pallas_call(functools.partial(pipeline_kernel, sections), out_shape=ja...  186 us
    reduce_scatter x1, waiting for transfers between devices, per_device(): lax.psum_scatter(both, 'dp', scatter_dimension=0, tiled=True).astype(F32)  75.3 us
  transfers between devices with their start and end apart: 1, of which 1 were waited for; matrix products, arithmetic and copies ran while one was open for 0% of the time, Pallas kernels for 0%

profile of v2, /device:TPU:1, one launch (start us, length us, event | category | flops | bytes accessed | tf_op | source)
XLA Modules:
  0.0 278.1 jit_solution(8691253132332353963)
XLA Ops:
  7.2 0.0 reduce-scatter.2.cloned.1.call-start
  7.2 186.1 %pipeline.1 = bf16[1280,2560]{1,0:T(8,128)(2,1)} custom-call(s32[4]{0:T(128)} %bitcast.11, s32[4]{0:T(128)} %arrival_ref.1, bf16[4,256,1280]{2,1,0:T(8,128)(2,1)} %bitcast.9, bf16[4,256,1280]{2,1,0:T(8,128)(2,1)} %cot_ref.1, f32[1,1280]{1,0:T(1,128)} %gain_ref.1, bf16[1280,1920]{1,0:T(8,128)(2,1)} %bitcast.8, bf16[1280,640]{1,0:T(8,128)(2,1)} %bitcast.10), custom_call_target="tpu_custom_call" | custom-call | tf_op jit(solution)/shard_map/pipeline/pallas_call | solution.py:339
  193.3 0.0 reduce-scatter.2.cloned.1.call-update
  193.4 75.3 %reduce-scatter.2.cloned.1.call-done = bf16[80,2560]{1,0:T(8,128)(2,1)} async-done(((bf16[1280,2560]{1,0:T(8,128)(2,1)}), bf16[80,2560]{1,0:T(8,128)(2,1)}) %reduce-scatter.2.cloned.1.call-update) | async-done | bytes 409616 | tf_op jit(solution)/shard_map/reduce_scatter | solution.py:365
  268.6 1.1 convert_element_type.3
  269.7 0.7 slice_bitcast_fusion.1
  270.4 0.9 slice_bitcast_fusion
Async XLA Ops:
  7.2 261.5 %reduce-scatter.2.cloned.1.call-start = ((), (), s32[]{:S(2)}) async-start(), calls=%async_computation.1 | async-start | bytes 6963200 | tf_op jit(solution)/shard_map/reduce_scatter | solution.py:365
Sparse Core Ops, SparseCore 0:
  193.5 75.0 reduce-scatter.1

commit v3 on v2

--- a/solution.py
+++ b/solution.py
@@ -11,6 +11,8 @@
 HEADS = 8
 EPSILON = 1e-06
 MESH = pl.DeviceIdType.MESH
+TILE = 256
+TX = 6
 F32 = jnp.float32
 BF16 = jnp.bfloat16
 
@@ -50,7 +52,8 @@
     gain_ref,
     wqkv_ref,
     wo_ref,
-    out_ref,
+    qkv_out,
+    out_out,
     wqkv_t,
     wo_t,
     gain_b,
@@ -67,13 +70,23 @@
     ga_acc,
     gpk_t,
     gain_w,
-    acc_q,
-    acc_o,
+    acc,
     g_recv,
     g_send,
     send_sem,
     recv_sem,
     go_sem,
+    stage,
+    got_a,
+    got_y1,
+    got_x1,
+    got_x2,
+    got_y2,
+    got_y3,
+    got_x3,
+    send_x3,
+    rs_send,
+    rs_recv,
 ):
     micro, slots, width = x_ref.shape
     head_span = wo_ref.shape[1]
@@ -85,11 +98,20 @@
     lane = lax.axis_index("dp")
     core = lax.rem(lane, 2)
     twin = lane + 1 - 2 * core
+    row = lax.rem(lane // 2, 2)
+    col = lane // 4
+    cols = stage.shape[1]
+    right, left, far = (lax.rem(col + step, cols) for step in (1, cols - 1, 2))
+    rest = row * 2 + core
+    to_right = right * 4 + rest
+    to_left = left * 4 + rest
+    to_row = col * 4 + (1 - row) * 2 + core
     barrier = pltpu.get_barrier_semaphore()
     for other in (below, above):
         pl.semaphore_signal(barrier, inc=1, device_id={"section": other}, device_id_type=MESH)
-    pl.semaphore_signal(barrier, inc=1, device_id={"dp": twin}, device_id_type=MESH)
-    pl.semaphore_wait(barrier, 3)
+    for other in (twin, to_right, to_left, to_row):
+        pl.semaphore_signal(barrier, inc=1, device_id={"dp": other}, device_id_type=MESH)
+    pl.semaphore_wait(barrier, 6)
 
     def turn_wo(c):
         wo_t[:, rows_at(c, 256)] = wo_ref[rows_at(c, 256), :].T
@@ -112,6 +134,9 @@
     CH = 160
     PIECE = 256
     pieces = width // PIECE
+    tiles = acc.shape[0]
+    whole = packed // TILE
+    edge = TILE - (packed - whole * TILE)
     chunks = width // CH
 
     def gain_rows(c, size):
@@ -242,24 +267,166 @@
 
         loop(pieces, grad_hidden)
 
+    def tile(p, n):
+        if isinstance(n, int) and n == whole:
+            half = dot_nt(hid_t[...], gpk_t[n * TILE : packed, :])
+            return jnp.concatenate([half, dot_nt(g_recv[p], attn_t[0:edge, :])], axis=1)
+        if isinstance(n, int) and n > whole:
+            start = edge + (n - whole - 1) * TILE
+            return dot_nt(g_recv[p], attn_t[start : start + TILE, :])
+        return dot_nt(hid_t[...], gpk_t[rows_at(n, TILE), :])
+
     def weights(p):
         def qkv(n):
-            acc_q[:, rows_at(n, 256)] += dot_nt(hid_t[...], gpk_t[rows_at(n, 256), :])
-
-        loop(packed // 256, qkv)
-        tail = packed // 256 * 256
-        acc_q[:, tail:packed] += dot_nt(hid_t[...], gpk_t[tail:packed, :])
-
-        def out(n):
-            acc_o[:, rows_at(n, 256)] += dot_nt(g_recv[p], attn_t[rows_at(n, 256), :])
-
-        loop(head_span // 256, out)
-        tail = head_span // 256 * 256
-        acc_o[:, tail:head_span] += dot_nt(g_recv[p], attn_t[tail:head_span, :])
+            acc[n] += tile(p, n)
+
+        loop(whole, qkv)
+        for n in range(whole, tiles):
+            acc[n] += tile(p, n)
+
+    def give_twin(n):
+        return send(stage.at[n, :, :, 1 - core], got_a.at[n], n, twin)
+
+    def send(src, dst, i, lane_to):
+        return pltpu.make_async_remote_copy(
+            src_ref=src,
+            dst_ref=dst,
+            send_sem=rs_send.at[i],
+            recv_sem=rs_recv.at[i],
+            device_id={"dp": lane_to},
+            device_id_type=MESH,
+        )
+
+    def last_weights(p):
+        def put(n):
+            total = (acc[n] + tile(p, n)).astype(BF16)
+            stage[n] = total.reshape(stage.shape[1:])
+            give_twin(n).start()
+
+        for n in range(whole, tiles):
+            put(n)
+
+        def qkv(i):
+            put(whole - 1 - i)
+
+        loop(whole, qkv)
+
+    def join(at, other):
+        stage[at] = (stage[at].astype(F32) + other.astype(F32)).astype(BF16)
+
+    def reduce_out():
+        nx, ny = TX, tiles - TX
+        hx, hy = nx // 2, ny // 2
+        xa, xb = pl.ds(0, hx), pl.ds(hx, nx - hx)
+        ya, yb = pl.ds(nx, hy), pl.ds(nx + hy, ny - hy)
+        base = tiles
+        y1 = [
+            send(stage.at[nx + i, :, 1 - row, core], got_y1.at[i], base + i, to_row)
+            for i in range(ny)
+        ]
+        base += ny
+        x1 = (
+            send(stage.at[xa, far, :, core], got_x1.at[0, 0:hx], base, to_right),
+            send(stage.at[xb, far, :, core], got_x1.at[1, 0 : nx - hx], base + 1, to_left),
+        )
+        x2a = (
+            send(stage.at[xb, right, :, core], got_x2.at[0, hx:nx], base + 2, to_right),
+            send(stage.at[xa, left, :, core], got_x2.at[1, 0:hx], base + 3, to_left),
+        )
+        x2b = (
+            send(stage.at[xa, right, :, core], got_x2.at[0, 0:hx], base + 4, to_right),
+            send(stage.at[xb, left, :, core], got_x2.at[1, hx:nx], base + 5, to_left),
+        )
+        y2 = (
+            send(stage.at[ya, far, row, core], got_y2.at[0, 0:hy], base + 6, to_right),
+            send(stage.at[yb, far, row, core], got_y2.at[1, 0 : ny - hy], base + 7, to_left),
+        )
+        y3a = (
+            send(stage.at[yb, right, row, core], got_y3.at[0, hy:ny], base + 8, to_right),
+            send(stage.at[ya, left, row, core], got_y3.at[1, 0:hy], base + 9, to_left),
+        )
+        y3b = (
+            send(stage.at[ya, right, row, core], got_y3.at[0, 0:hy], base + 10, to_right),
+            send(stage.at[yb, left, row, core], got_y3.at[1, hy:ny], base + 11, to_left),
+        )
+        x3 = send(send_x3, got_x3, base + 12, to_row)
+
+        def meet(n):
+            give_twin(n).wait_recv()
+            for c in range(cols):
+                join((n, c, slice(None), core), got_a[n, c])
+
+        for i in reversed(range(ny)):
+            meet(nx + i)
+            y1[i].start()
+
+        def meet_x(i):
+            meet(nx - 1 - i)
+
+        loop(nx, meet_x)
+        for copy in x1 + x2a:
+            copy.start()
+        for i in range(ny):
+            y1[i].wait_recv()
+            for c in range(cols):
+                join((nx + i, c, row, core), got_y1[i, c])
+        x1[0].wait_recv()
+        for i in range(hx):
+            join((i, right, slice(None), core), got_x1[0, i])
+        x2b[0].start()
+        x1[1].wait_recv()
+        for i in range(nx - hx):
+            join((hx + i, left, slice(None), core), got_x1[1, i])
+        x2b[1].start()
+        for copy in y2 + y3a:
+            copy.start()
+        y2[0].wait_recv()
+        for i in range(hy):
+            join((nx + i, right, row, core), got_y2[0, i])
+        y3b[0].start()
+        y2[1].wait_recv()
+        for i in range(ny - hy):
+            join((nx + hy + i, left, row, core), got_y2[1, i])
+        y3b[1].start()
+
+        def across(n, r):
+            total = stage[n, col, r, core].astype(F32) + got_x2[0, n, r].astype(F32)
+            return total + got_x2[1, n, r].astype(F32)
+
+        for copy in x2a + x2b:
+            copy.wait_recv()
+        for n in range(nx):
+            send_x3[n] = across(n, 1 - row).astype(BF16)
+        x3.start()
+
+        def emit(n, value):
+            if n < whole:
+                qkv_out[:, n * TILE : (n + 1) * TILE] = value
+            elif n == whole:
+                qkv_out[:, n * TILE : packed] = value[:, : TILE - edge]
+                out_out[:, 0:edge] = value[:, TILE - edge :]
+            else:
+                start = edge + (n - whole - 1) * TILE
+                out_out[:, start : start + TILE] = value
+
+        for copy in y3a + y3b:
+            copy.wait_recv()
+        for i in range(ny):
+            total = stage[nx + i, col, row, core].astype(F32) + got_y3[0, i].astype(F32)
+            emit(nx + i, total + got_y3[1, i].astype(F32))
+        x3.wait_recv()
+        for n in range(nx):
+            emit(n, across(n, row) + got_x3[n].astype(F32))
+        for copy in tuple(y1) + x1 + x2a + x2b + y2 + y3a + y3b + (x3,):
+            copy.wait_send()
+
+        def given(n):
+            give_twin(n).wait_send()
+
+        loop(tiles, given)
 
     def clear(c):
-        acc_q[rows_at(c, 64), :] = jnp.zeros((64, packed), F32)
-        acc_o[rows_at(c, 64), :] = jnp.zeros((64, head_span), F32)
+        acc[:, rows_at(c, 32), :] = jnp.zeros((tiles, 32, TILE), F32)
 
     forward(0)
     loop(packed // 480, weigh)
@@ -277,9 +444,15 @@
 
         @pl.when(p == 0)
         def _():
-            loop(width // 64, clear)
-
-        weights(p)
+            loop(width // 32, clear)
+
+        @pl.when(p < micro - 1)
+        def _():
+            weights(p)
+
+        @pl.when(p == micro - 1)
+        def _():
+            last_weights(p)
 
         @pl.when((sec == sections - 1) & (p == 0) & (core == 0))
         def _():
@@ -290,6 +463,7 @@
             forward(p + 1)
 
     loop(micro, moment)
+    reduce_out()
 
     @pl.when(sec > 0)
     def _():
@@ -299,16 +473,11 @@
 
         loop(micro, drain)
 
-    def finish(c):
-        out_ref[rows_at(c, 64), 0:packed] = acc_q[rows_at(c, 64), :].astype(BF16)
-        out_ref[rows_at(c, 64), packed:] = acc_o[rows_at(c, 64), :].astype(BF16)
-
-    loop(width // 64, finish)
-
-
-def run_pipeline(sections, counts, arrival, x, cotangent, gain, wqkv, wo):
+
+def run_pipeline(sections, lanes, counts, arrival, x, cotangent, gain, wqkv, wo):
     micro, slots, width = x.shape
     packed, head_span = wqkv.shape[1], wo.shape[1]
+    tiles, cols, share = (packed + head_span) // TILE, lanes // 4, width // lanes
     vmem = pl.BlockSpec(memory_space=pltpu.VMEM)
     smem = pl.BlockSpec(memory_space=pltpu.SMEM)
     scratch = [
@@ -328,19 +497,32 @@
         pltpu.VMEM((head_span, slots), F32),
         pltpu.VMEM((packed, slots), BF16),
         pltpu.VMEM((packed, 128), F32),
-        pltpu.VMEM((width, packed), F32),
-        pltpu.VMEM((width, head_span), F32),
+        pltpu.VMEM((tiles, width, TILE), F32),
         pltpu.VMEM((micro, width, slots), BF16),
         pltpu.VMEM((micro, width, slots), BF16),
         pltpu.SemaphoreType.DMA((micro, width // 256)),
         pltpu.SemaphoreType.DMA((micro, width // 256)),
         pltpu.SemaphoreType.REGULAR,
+        pltpu.VMEM((tiles, cols, 2, 2, share, TILE), BF16),
+        pltpu.VMEM((tiles, cols, 2, share, TILE), BF16),
+        pltpu.VMEM((tiles - TX, cols, share, TILE), BF16),
+        pltpu.VMEM((2, TX - TX // 2, 2, share, TILE), BF16),
+        pltpu.VMEM((2, TX, 2, share, TILE), BF16),
+        pltpu.VMEM((2, tiles - TX - (tiles - TX) // 2, share, TILE), BF16),
+        pltpu.VMEM((2, tiles - TX, share, TILE), BF16),
+        pltpu.VMEM((TX, share, TILE), BF16),
+        pltpu.VMEM((TX, share, TILE), BF16),
+        pltpu.SemaphoreType.DMA((tiles + tiles - TX + 13,)),
+        pltpu.SemaphoreType.DMA((tiles + tiles - TX + 13,)),
     ]
     return pl.pallas_call(
         functools.partial(pipeline_kernel, sections),
-        out_shape=jax.ShapeDtypeStruct((width, packed + head_span), BF16),
+        out_shape=(
+            jax.ShapeDtypeStruct((share, packed), F32),
+            jax.ShapeDtypeStruct((share, head_span), F32),
+        ),
         in_specs=[smem, smem, vmem, vmem, vmem, vmem, vmem],
-        out_specs=vmem,
+        out_specs=(vmem, vmem),
         scratch_shapes=scratch,
         compiler_params=pltpu.CompilerParams(
             collective_id=0, has_side_effects=True, vmem_limit_bytes=64 * 1024 * 1024 - 65536
@@ -351,9 +533,9 @@
 
 def per_device(activations, cotangent, counts, arrival, norm_gain, qkv_weight, out_weight):
     sections = lax.axis_size("section")
-    packed = qkv_weight.shape[2]
-    both = run_pipeline(
+    qkv_share, out_share = run_pipeline(
         sections,
+        lax.axis_size("dp"),
         counts[:, 0],
         arrival,
         activations[0],
@@ -362,8 +544,7 @@
         qkv_weight[0],
         out_weight[0],
     )
-    share = lax.psum_scatter(both, "dp", scatter_dimension=0, tiled=True).astype(F32)
-    return (share[None, :, :packed], share[None, :, packed:])
+    return (qkv_share[None], out_share[None])
 
 
 def solution(mesh):

time: 278 us -> 223 us (0.80)
  waiting for transfers between devices: 75.3 us -> 0 us
  Pallas kernels: 186 us -> 218 us
  between operations: 14 us -> 0.64 us
    reduce_scatter x1 -> x0, waiting for transfers between devices: 75.3 us -> none  [per_device(): lax.psum_scatter(both, 'dp', scatter_dimension=0, tiled=True).astype(F32)]
    pallas_call x1, Pallas kernels: 186 us -> 218 us  [run_pipeline(): pl.pallas_call(functools.partial(pipeline_kernel, sections), out_shape=(j...]
    unnamed x0 -> x2, local copies, waits for them, and re-layouts: none -> 3.56 us
  transfers between devices with their start and end apart: 1 -> 0, of which waited for: 1 -> 0; matrix products, arithmetic and copies ran while one was open for 0% -> 0% of each run, Pallas kernels for 0% -> 0%
where the time goes in v3:
time: 223 us; the launch traced here: 222 us
  Pallas kernels  218 us (98%)
  local copies, waits for them, and re-layouts  3.56 us (2%)
    pallas_call x1, Pallas kernels, run_pipeline(): pl.pallas_call(functools.partial(pipeline_kernel, sections), out_shape=(j...  218 us

profile of v3, /device:TPU:1, one launch (start us, length us, event | category | flops | bytes accessed | tf_op | source)
XLA Modules:
  0.0 222.5 jit_solution(2496786161688798056)
XLA Ops:
  0.6 218.3 %pipeline.1 = (f32[80,1920]{1,0:T(8,128)}, f32[80,640]{1,0:T(8,128)}) custom-call(s32[4]{0:T(128)} %bitcast.11, s32[4]{0:T(128)} %arrival_ref.1, bf16[4,256,1280]{2,1,0:T(8,128)(2,1)} %bitcast.7, bf16[4,256,1280]{2,1,0:T(8,128)(2,1)} %cot_ref.1, f32[1,1280]{1,0:T(1,128)} %gain_ref.1, bf16[1280,1920]{1,0:T(8,128)(2,1)} %bitcast.6, bf16[1280,640]{1,0:T(8,128)(2,1)} %bitcast.8), custom_call_target="tpu_custom_call" | custom-call | tf_op jit(solution)/shard_map/pipeline/pallas_call | solution.py:518
  218.9 1.9 copy.11
  220.9 1.6 copy.12

commit v4 on v3

--- a/solution.py
+++ b/solution.py
@@ -12,7 +12,9 @@
 EPSILON = 1e-06
 MESH = pl.DeviceIdType.MESH
 TILE = 256
+PIECE = 256
 TX = 6
+TURN = 2
 F32 = jnp.float32
 BF16 = jnp.bfloat16
 
@@ -47,35 +49,36 @@
     sections,
     counts_ref,
     arrival_ref,
+    x_hbm,
+    cot_hbm,
+    gain_ref,
+    wqkv_hbm,
+    wo_hbm,
+    qkv_out,
+    out_out,
     x_ref,
     cot_ref,
-    gain_ref,
     wqkv_ref,
-    wo_ref,
-    qkv_out,
-    out_out,
     wqkv_t,
     wo_t,
     gain_b,
+    gain_w,
     x_t,
-    norm_t,
     hid_t,
     stats,
     pk_t,
-    v_n,
-    prob_f,
     prob_h,
     attn_t,
     ga_t,
     ga_acc,
     gpk_t,
-    gain_w,
     acc,
     g_recv,
     g_send,
     send_sem,
     recv_sem,
     go_sem,
+    load_sem,
     stage,
     got_a,
     got_y1,
@@ -89,9 +92,13 @@
     rs_recv,
 ):
     micro, slots, width = x_ref.shape
-    head_span = wo_ref.shape[1]
+    head_span = wo_hbm.shape[1]
     packed = wqkv_ref.shape[1]
     scale = HDIM**-0.5
+    pieces = width // PIECE
+    tiles = acc.shape[0]
+    whole = packed // TILE
+    edge = TILE - (packed - whole * TILE)
     sec = lax.axis_index("section")
     below = lax.rem(sec + sections - 1, sections)
     above = lax.rem(sec + 1, sections)
@@ -106,104 +113,127 @@
     to_right = right * 4 + rest
     to_left = left * 4 + rest
     to_row = col * 4 + (1 - row) * 2 + core
+    top = sec == sections - 1
+
+    def load(src, dst, i):
+        return pltpu.make_async_copy(src, dst, load_sem.at[i])
+
+    def load_cot(p):
+        return load(cot_hbm.at[p], cot_ref, 0)
+
+    load_x = load(x_hbm, x_ref, 1)
+    load_w = [
+        load(wqkv_hbm.at[rows_at(c, PIECE)], wqkv_ref.at[rows_at(c, PIECE)], 2 + c)
+        for c in range(pieces)
+    ]
+    wo_parts = [(at, min(PIECE, head_span - at)) for at in range(0, head_span, PIECE)]
+    load_wo = [
+        load(
+            wo_hbm.at[:, pl.ds(at, size)],
+            hid_t.at[1 + i, :, pl.ds(0, size)],
+            2 + pieces + i,
+        )
+        for i, (at, size) in enumerate(wo_parts)
+    ]
+    load_x.start()
+    for copy in load_w + load_wo:
+        copy.start()
+
+    @pl.when(top)
+    def _():
+        load_cot(0).start()
+
     barrier = pltpu.get_barrier_semaphore()
     for other in (below, above):
         pl.semaphore_signal(barrier, inc=1, device_id={"section": other}, device_id_type=MESH)
     for other in (twin, to_right, to_left, to_row):
         pl.semaphore_signal(barrier, inc=1, device_id={"dp": other}, device_id_type=MESH)
     pl.semaphore_wait(barrier, 6)
-
-    def turn_wo(c):
-        wo_t[:, rows_at(c, 256)] = wo_ref[rows_at(c, 256), :].T
-
-    def turn_wqkv(c):
-        wqkv_t[:, rows_at(c, 256)] = wqkv_ref[rows_at(c, 256), :].T
-
-    loop(width // 256, turn_wqkv)
-    loop(width // 256, turn_wo)
     gain_b[...] = jnp.broadcast_to(gain_ref[...], (128, width)).T
-
-    gain_hi = gain_b[...].astype(BF16)
-    gain_lo = (gain_b[...] - gain_hi.astype(F32)).astype(BF16)
-    gains = jnp.concatenate([gain_hi, gain_lo], axis=1)
-
-    def weigh(m):
-        both = dot_nn(wqkv_t[rows_at(m, 480), :], gains) * (1.0 / width)
-        gain_w[rows_at(m, 480), :] = both[:, :128] + both[:, 128:]
+    load_x.wait()
+
+    def turn_weights():
+        for c in range(pieces):
+            load_w[c].wait()
+            wqkv_t[:, rows_at(c, PIECE)] = wqkv_ref[rows_at(c, PIECE), :].T
+        for i, (at, size) in enumerate(wo_parts):
+            load_wo[i].wait()
+            wo_t[at : at + size, :] = hid_t[1 + i, :, 0:size].T
+        gain_hi = gain_b[...].astype(BF16)
+        gain_lo = (gain_b[...] - gain_hi.astype(F32)).astype(BF16)
+        gains = jnp.concatenate([gain_hi, gain_lo], axis=1)
+
+        def weigh(m):
+            both = dot_nn(wqkv_t[rows_at(m, 480), :], gains) * (1.0 / width)
+            gain_w[rows_at(m, 480), :] = both[:, :128] + both[:, 128:]
+
+        loop(packed // 480, weigh)
 
     CH = 160
-    PIECE = 256
-    pieces = width // PIECE
-    tiles = acc.shape[0]
-    whole = packed // TILE
-    edge = TILE - (packed - whole * TILE)
     chunks = width // CH
 
     def gain_rows(c, size):
         part = gain_b[rows_at(c, size), :]
         return jnp.concatenate([part] * (slots // 128), axis=1)
 
-    def forward(p):
+    def normalize(p):
         chosen = arrival_ref[p]
-        count = counts_ref[chosen]
 
         def turn(c, total):
-            piece = x_ref[chosen, :, rows_at(c, 256)].T
-            x_t[rows_at(c, 256), :] = piece
+            piece = x_ref[chosen, :, rows_at(c, PIECE)].T
+            x_t[p, rows_at(c, PIECE), :] = piece
             return total + fold(piece.astype(F32))
 
         zero = jnp.zeros((8, slots), F32)
-        total = lax.fori_loop(0, width // 256, turn, zero)
+        total = lax.fori_loop(0, pieces, turn, zero)
         mean = jnp.sum(total, axis=0, keepdims=True) * (1.0 / width)
 
         def add_sq(c, total):
-            centered = x_t[rows_at(c, 320), :].astype(F32) - mean
+            centered = x_t[p, rows_at(c, 320), :].astype(F32) - mean
             return total + fold(centered * centered)
 
         total = lax.fori_loop(0, width // 320, add_sq, zero)
         var = jnp.sum(total, axis=0, keepdims=True) * (1.0 / width)
         inv = lax.rsqrt(var + EPSILON)
-        stats[0:1, :] = inv
+        stats[p, 0:1, :] = inv
+        stats[p, 1:2, :] = mean
+
+    def attend(p):
+        count = counts_ref[arrival_ref[p]]
+        inv = stats[p, 0:1, :]
+        mean = stats[p, 1:2, :]
 
         def norm(c):
-            normed = (x_t[rows_at(c, CH), :].astype(F32) - mean) * inv
-            norm_t[rows_at(c, CH), :] = normed
-            hid_t[rows_at(c, CH), :] = (normed * gain_rows(c, CH)).astype(BF16)
+            normed = (x_t[p, rows_at(c, CH), :].astype(F32) - mean) * inv
+            hid_t[p, rows_at(c, CH), :] = (normed * gain_rows(c, CH)).astype(BF16)
 
         loop(chunks, norm)
 
         def pack(m):
-            pk_t[rows_at(m, 480), :] = dot_nn(wqkv_t[rows_at(m, 480), :], hid_t[...]).astype(BF16)
+            part = dot_nn(wqkv_t[rows_at(m, 480), :], hid_t[p])
+            pk_t[p, rows_at(m, 480), :] = part.astype(BF16)
 
         loop(packed // 480, pack)
         keep = lax.broadcasted_iota(jnp.int32, (slots, slots), 0) < count
-
-        def head(h):
-            q = pk_t[rows_at(h, HDIM), :]
-            k = pk_t[rows_at(h + HEADS, HDIM), :]
-            v = pk_t[rows_at(h + 2 * HEADS, HDIM), :]
-            s = dot_nn(k.T, q) * scale
-            s = jnp.where(keep, s, -1e30)
+        for h in range(HEADS):
+            q = pk_t[p, rows_at(h, HDIM), :]
+            k = pk_t[p, rows_at(h + HEADS, HDIM), :]
+            v = pk_t[p, rows_at(h + 2 * HEADS, HDIM), :]
+            s = jnp.where(keep, dot_nn(k.T, q) * scale, -1e30)
             e = jnp.exp(s - jnp.max(s, axis=0, keepdims=True))
-            prob = e * (1.0 / jnp.sum(e, axis=0, keepdims=True))
-            prob_f[h] = prob
-            half = prob.astype(BF16)
-            prob_h[h] = half
-            v_n[h] = v.T
-            attn_t[rows_at(h, HDIM), :] = dot_nn(v, half).astype(BF16)
-
-        for h in range(HEADS):
-            head(h)
+            half = (e * (1.0 / jnp.sum(e, axis=0, keepdims=True))).astype(BF16)
+            prob_h[p, h] = half
+            attn_t[p, rows_at(h, HDIM), :] = dot_nn(v, half).astype(BF16)
 
     def take_cotangent(p, c):
         count = counts_ref[arrival_ref[p]]
         keep = (lax.broadcasted_iota(jnp.int32, (1, slots), 1) < count).astype(F32)
-        piece = cot_ref[p, :, rows_at(c, PIECE)].T.astype(F32) * keep
+        piece = cot_ref[:, rows_at(c, PIECE)].T.astype(F32) * keep
         g_recv[p, rows_at(c, PIECE), :] = piece.astype(BF16)
 
     def hop(p, c):
         return pltpu.make_async_remote_copy(
-            src_ref=g_send.at[p, rows_at(c, PIECE)],
+            src_ref=g_send.at[lax.rem(p, 2), rows_at(c, PIECE)],
             dst_ref=g_recv.at[p, rows_at(c, PIECE)],
             send_sem=send_sem.at[p, c],
             recv_sem=recv_sem.at[p, c],
@@ -212,13 +242,17 @@
         )
 
     def backward(p):
+        @pl.when(top)
+        def _():
+            load_cot(p).wait()
+
         for c in range(pieces):
 
-            @pl.when(sec == sections - 1)
+            @pl.when(top)
             def _():
                 take_cotangent(p, c)
 
-            @pl.when(sec < sections - 1)
+            @pl.when(jnp.logical_not(top))
             def _():
                 hop(p, c).wait_recv()
 
@@ -230,23 +264,28 @@
             else:
                 ga_t[...] = (ga_acc[...] + part).astype(BF16)
 
+        @pl.when(top & (p < micro - 1))
+        def _():
+            load_cot(p + 1).start()
+
         first = jnp.zeros((8, slots), F32)
         second = jnp.zeros((8, slots), F32)
         for h in range(HEADS):
-            q = pk_t[rows_at(h, HDIM), :]
-            k = pk_t[rows_at(h + HEADS, HDIM), :]
-            v = pk_t[rows_at(h + 2 * HEADS, HDIM), :]
+            q = pk_t[p, rows_at(h, HDIM), :]
+            k = pk_t[p, rows_at(h + HEADS, HDIM), :]
+            v = pk_t[p, rows_at(h + 2 * HEADS, HDIM), :]
             ga = ga_t[rows_at(h, HDIM), :]
-            prob = prob_f[h]
-            grad_prob = dot_nn(v_n[h], ga)
+            half = prob_h[p, h]
+            prob = half.astype(F32)
+            grad_prob = dot_nn(v.T, ga)
             inner = jnp.sum(prob * grad_prob, axis=0, keepdims=True)
             gs = (prob * (grad_prob - inner) * scale).astype(BF16)
-            grads = (dot_nn(k, gs), dot_nt(q, gs), dot_nt(ga, prob_h[h]))
+            grads = (dot_nn(k, gs), dot_nt(q, gs), dot_nt(ga, half))
             for i, (grad, own) in enumerate(zip(grads, (q, k, v))):
                 at = rows_at(h + i * HEADS, HDIM)
-                half = grad.astype(BF16)
-                gpk_t[at, :] = half
-                full = half.astype(F32)
+                rounded = grad.astype(BF16)
+                gpk_t[at, :] = rounded
+                full = rounded.astype(F32)
                 w = gain_w[at, :]
                 first += fold(full * jnp.concatenate([w] * (slots // 128), axis=1))
                 second += fold(full * own.astype(F32))
@@ -256,25 +295,33 @@
         )
 
     def pass_down(p, first, second):
-        inv = stats[0:1, :]
+        inv = stats[p, 0:1, :]
+        mean = stats[p, 1:2, :]
+
+        @pl.when(p >= 2)
+        def _():
+            for c in range(pieces):
+                if c != TURN:
+                    hop(p - 2, c).wait_send()
 
         def grad_hidden(c):
             at = rows_at(c, PIECE)
             gn = dot_nn(wqkv_ref[at, :], gpk_t[...]) * gain_rows(c, PIECE)
-            grad_ln = inv * (gn - first - norm_t[at, :] * second)
-            g_send[p, at, :] = (g_recv[p, at, :].astype(F32) + grad_ln).astype(BF16)
+            normed = (x_t[p, at, :].astype(F32) - mean) * inv
+            grad_ln = inv * (gn - first - normed * second)
+            g_send[lax.rem(p, 2), at, :] = (g_recv[p, at, :].astype(F32) + grad_ln).astype(BF16)
             hop(p, c).start()
 
         loop(pieces, grad_hidden)
 
     def tile(p, n):
         if isinstance(n, int) and n == whole:
-            half = dot_nt(hid_t[...], gpk_t[n * TILE : packed, :])
-            return jnp.concatenate([half, dot_nt(g_recv[p], attn_t[0:edge, :])], axis=1)
+            half = dot_nt(hid_t[p], gpk_t[n * TILE : packed, :])
+            return jnp.concatenate([half, dot_nt(g_recv[p], attn_t[p, 0:edge, :])], axis=1)
         if isinstance(n, int) and n > whole:
             start = edge + (n - whole - 1) * TILE
-            return dot_nt(g_recv[p], attn_t[start : start + TILE, :])
-        return dot_nt(hid_t[...], gpk_t[rows_at(n, TILE), :])
+            return dot_nt(g_recv[p], attn_t[p, start : start + TILE, :])
+        return dot_nt(hid_t[p], gpk_t[rows_at(n, TILE), :])
 
     def weights(p):
         def qkv(n):
@@ -428,13 +475,24 @@
     def clear(c):
         acc[:, rows_at(c, 32), :] = jnp.zeros((tiles, 32, TILE), F32)
 
-    forward(0)
-    loop(packed // 480, weigh)
+    ahead = jnp.minimum(micro, 1 + 2 * (sections - 1 - sec))
+
+    def early(p, carry):
+        normalize(p)
+
+        @pl.when(p == 0)
+        def _():
+            turn_weights()
+
+        attend(p)
+        return carry
+
+    lax.fori_loop(0, ahead, early, 0)
 
     def moment(p):
         sums = backward(p)
 
-        @pl.when((sec == sections - 1) & (p == 0) & (core == 1))
+        @pl.when((sec > 0) & ((core == 0) | (p > 0)))
         def _():
             pl.semaphore_wait(go_sem, 1)
 
@@ -454,24 +512,29 @@
         def _():
             last_weights(p)
 
-        @pl.when((sec == sections - 1) & (p == 0) & (core == 0))
-        def _():
+        @pl.when((sec > 0) & ((core == 1) | (p < micro - 1)))
+        def _():
+            hop(p, TURN).wait_send()
             pl.semaphore_signal(go_sem, inc=1, device_id={"dp": twin}, device_id_type=MESH)
 
-        @pl.when(p < micro - 1)
-        def _():
-            forward(p + 1)
+        @pl.when(p + ahead < micro)
+        def _():
+            normalize(p + ahead)
+            attend(p + ahead)
 
     loop(micro, moment)
     reduce_out()
 
     @pl.when(sec > 0)
     def _():
-        def drain(p):
+        for p in range(micro - 2, micro):
             for c in range(pieces):
-                hop(p, c).wait_send()
-
-        loop(micro, drain)
+                if c != TURN:
+                    hop(p, c).wait_send()
+
+    @pl.when((sec > 0) & (core == 0))
+    def _():
+        hop(micro - 1, TURN).wait_send()
 
 
 def run_pipeline(sections, lanes, counts, arrival, x, cotangent, gain, wqkv, wo):
@@ -480,29 +543,32 @@
     tiles, cols, share = (packed + head_span) // TILE, lanes // 4, width // lanes
     vmem = pl.BlockSpec(memory_space=pltpu.VMEM)
     smem = pl.BlockSpec(memory_space=pltpu.SMEM)
+    hbm = pl.BlockSpec(memory_space=pl.ANY)
+    pieces = width // PIECE
     scratch = [
+        pltpu.VMEM((micro, slots, width), BF16),
+        pltpu.VMEM((slots, width), BF16),
+        pltpu.VMEM((width, packed), BF16),
         pltpu.VMEM((packed, width), BF16),
         pltpu.VMEM((head_span, width), BF16),
         pltpu.VMEM((width, 128), F32),
-        pltpu.VMEM((width, slots), BF16),
-        pltpu.VMEM((width, slots), F32),
-        pltpu.VMEM((width, slots), BF16),
-        pltpu.VMEM((8, slots), F32),
-        pltpu.VMEM((packed, slots), BF16),
-        pltpu.VMEM((HEADS, slots, HDIM), BF16),
-        pltpu.VMEM((HEADS, slots, slots), F32),
-        pltpu.VMEM((HEADS, slots, slots), BF16),
-        pltpu.VMEM((head_span, slots), BF16),
+        pltpu.VMEM((packed, 128), F32),
+        pltpu.VMEM((micro, width, slots), BF16),
+        pltpu.VMEM((micro, width, slots), BF16),
+        pltpu.VMEM((micro, 8, slots), F32),
+        pltpu.VMEM((micro, packed, slots), BF16),
+        pltpu.VMEM((micro, HEADS, slots, slots), BF16),
+        pltpu.VMEM((micro, head_span, slots), BF16),
         pltpu.VMEM((head_span, slots), BF16),
         pltpu.VMEM((head_span, slots), F32),
         pltpu.VMEM((packed, slots), BF16),
-        pltpu.VMEM((packed, 128), F32),
         pltpu.VMEM((tiles, width, TILE), F32),
         pltpu.VMEM((micro, width, slots), BF16),
-        pltpu.VMEM((micro, width, slots), BF16),
-        pltpu.SemaphoreType.DMA((micro, width // 256)),
-        pltpu.SemaphoreType.DMA((micro, width // 256)),
+        pltpu.VMEM((2, width, slots), BF16),
+        pltpu.SemaphoreType.DMA((micro, pieces)),
+        pltpu.SemaphoreType.DMA((micro, pieces)),
         pltpu.SemaphoreType.REGULAR,
+        pltpu.SemaphoreType.DMA((2 + pieces + -(-head_span // PIECE),)),
         pltpu.VMEM((tiles, cols, 2, 2, share, TILE), BF16),
         pltpu.VMEM((tiles, cols, 2, share, TILE), BF16),
         pltpu.VMEM((tiles - TX, cols, share, TILE), BF16),
@@ -521,7 +587,7 @@
             jax.ShapeDtypeStruct((share, packed), F32),
             jax.ShapeDtypeStruct((share, head_span), F32),
         ),
-        in_specs=[smem, smem, vmem, vmem, vmem, vmem, vmem],
+        in_specs=[smem, smem, hbm, hbm, vmem, hbm, hbm],
         out_specs=(vmem, vmem),
         scratch_shapes=scratch,
         compiler_params=pltpu.CompilerParams(

time: 223 us -> 207 us (0.928); the launches traced: 222 us -> 203 us
  Pallas kernels: 218 us -> 199 us
    pallas_call x1, Pallas kernels: 218 us -> 199 us  [run_pipeline(): pl.pallas_call(functools.partial(pipeline_kernel, sections), out_shape=(j...]
where the time goes in v4:
time: 207 us; the launch traced here: 203 us
  Pallas kernels  199 us (96%)
  local copies, waits for them, and re-layouts  3.56 us (2%)
    pallas_call x1, Pallas kernels, run_pipeline(): pl.pallas_call(functools.partial(pipeline_kernel, sections), out_shape=(j...  199 us

profile of v4, /device:TPU:1, one launch (start us, length us, event | category | flops | bytes accessed | tf_op | source)
XLA Modules:
  0.0 202.8 jit_solution(787316321987636336)
XLA Ops:
  0.6 198.6 %pipeline.1 = (f32[80,1920]{1,0:T(8,128)}, f32[80,640]{1,0:T(8,128)}) custom-call(s32[4]{0:T(128)} %bitcast.11, s32[4]{0:T(128)} %arrival_ref.1, bf16[4,256,1280]{2,1,0:T(8,128)(2,1)} %bitcast.7, bf16[4,256,1280]{2,1,0:T(8,128)(2,1)} %cot_hbm.1, f32[1,1280]{1,0:T(1,128)} %gain_ref.1, bf16[1280,1920]{1,0:T(8,128)(2,1)} %bitcast.6, bf16[1280,640]{1,0:T(8,128)(2,1)} %bitcast.8), custom_call_target="tpu_custom_call" | custom-call | tf_op jit(solution)/shard_map/pipeline/pallas_call | solution.py:584
  199.2 1.9 copy.11
  201.2 1.6 copy.12

commit v5 on v4

--- a/solution.py
+++ b/solution.py
@@ -54,8 +54,7 @@
     gain_ref,
     wqkv_hbm,
     wo_hbm,
-    qkv_out,
-    out_out,
+    out_ref,
     x_ref,
     cot_ref,
     wqkv_ref,
@@ -219,8 +218,8 @@
             q = pk_t[p, rows_at(h, HDIM), :]
             k = pk_t[p, rows_at(h + HEADS, HDIM), :]
             v = pk_t[p, rows_at(h + 2 * HEADS, HDIM), :]
-            s = jnp.where(keep, dot_nn(k.T, q) * scale, -1e30)
-            e = jnp.exp(s - jnp.max(s, axis=0, keepdims=True))
+            s = jnp.where(keep, dot_nn(k.T, q), -1e30)
+            e = jnp.exp((s - jnp.max(s, axis=0, keepdims=True)) * scale)
             half = (e * (1.0 / jnp.sum(e, axis=0, keepdims=True))).astype(BF16)
             prob_h[p, h] = half
             attn_t[p, rows_at(h, HDIM), :] = dot_nn(v, half).astype(BF16)
@@ -279,8 +278,8 @@
             prob = half.astype(F32)
             grad_prob = dot_nn(v.T, ga)
             inner = jnp.sum(prob * grad_prob, axis=0, keepdims=True)
-            gs = (prob * (grad_prob - inner) * scale).astype(BF16)
-            grads = (dot_nn(k, gs), dot_nt(q, gs), dot_nt(ga, half))
+            gs = (prob * (grad_prob - inner)).astype(BF16)
+            grads = (dot_nn(k, gs) * scale, dot_nt(q, gs) * scale, dot_nt(ga, half))
             for i, (grad, own) in enumerate(zip(grads, (q, k, v))):
                 at = rows_at(h + i * HEADS, HDIM)
                 rounded = grad.astype(BF16)
@@ -331,9 +330,6 @@
         for n in range(whole, tiles):
             acc[n] += tile(p, n)
 
-    def give_twin(n):
-        return send(stage.at[n, :, :, 1 - core], got_a.at[n], n, twin)
-
     def send(src, dst, i, lane_to):
         return pltpu.make_async_remote_copy(
             src_ref=src,
@@ -344,133 +340,153 @@
             device_id_type=MESH,
         )
 
+    nx, ny = TX, tiles - TX
+    hx, hy = nx // 2, ny // 2
+    at_y1 = tiles
+    at_x1 = at_y1 + ny
+    at_x2 = at_x1 + nx
+    at_x3 = at_x2 + 2 * nx
+    at_y2 = at_x3 + nx
+    at_y3 = at_y2 + ny
+    ways = ((to_right, right), (to_left, left))
+
+    def give_twin(n):
+        return send(stage.at[n, :, :, 1 - core], got_a.at[n], n, twin)
+
+    def copy_x1(n):
+        way = n // hx
+        return send(
+            stage.at[n, far, :, core], got_x1.at[way, n % hx], at_x1 + n, ways[way][0]
+        )
+
+    def copy_x2(way, n):
+        to, block = ways[way]
+        return send(stage.at[n, block, :, core], got_x2.at[way, n], at_x2 + way * nx + n, to)
+
+    def copy_x3(n):
+        return send(send_x3.at[n], got_x3.at[n], at_x3 + n, to_row)
+
+    def copy_y1(i):
+        return send(stage.at[nx + i, :, 1 - row, core], got_y1.at[i], at_y1 + i, to_row)
+
+    def copy_y2(i):
+        way = i // hy
+        return send(
+            stage.at[nx + i, far, row, core], got_y2.at[way, i % hy], at_y2 + i, ways[way][0]
+        )
+
+    def copy_y3(way, i):
+        to, block = ways[way]
+        return send(
+            stage.at[nx + i, block, row, core], got_y3.at[way, i], at_y3 + way * ny + i, to
+        )
+
+    def join(at, other):
+        stage[at] = (stage[at].astype(F32) + other.astype(F32)).astype(BF16)
+
+    def arrive(n):
+        give_twin(n).wait_recv()
+        for c in range(cols):
+            join((n, c, slice(None), core), got_a[n, c])
+        if n < nx:
+            copy_x1(n).start()
+            copy_x2(1 - n // hx, n).start()
+        else:
+            copy_y1(n - nx).start()
+
+    def x_second(n):
+        way = n // hx
+        copy_x1(n).wait_recv()
+        join((n, ways[way][1], slice(None), core), got_x1[way, n % hx])
+        copy_x2(way, n).start()
+
+    def across(n, r):
+        total = stage[n, col, r, core].astype(F32) + got_x2[0, n, r].astype(F32)
+        return total + got_x2[1, n, r].astype(F32)
+
+    def x_third(n):
+        copy_x2(0, n).wait_recv()
+        copy_x2(1, n).wait_recv()
+        send_x3[n] = across(n, 1 - row).astype(BF16)
+        copy_x3(n).start()
+
+    def x_last(n):
+        copy_x3(n).wait_recv()
+        out_ref[:, n * TILE : (n + 1) * TILE] = across(n, row) + got_x3[n].astype(F32)
+
+    def y_first(i):
+        copy_y1(i).wait_recv()
+        for c in range(cols):
+            join((nx + i, c, row, core), got_y1[i, c])
+        copy_y2(i).start()
+        copy_y3(1 - i // hy, i).start()
+
+    def y_second(i):
+        way = i // hy
+        copy_y2(i).wait_recv()
+        join((nx + i, ways[way][1], row, core), got_y2[way, i % hy])
+        copy_y3(way, i).start()
+
+    def y_last(i):
+        copy_y3(0, i).wait_recv()
+        copy_y3(1, i).wait_recv()
+        n = nx + i
+        total = stage[n, col, row, core].astype(F32) + got_y3[0, i].astype(F32)
+        out_ref[:, n * TILE : (n + 1) * TILE] = total + got_y3[1, i].astype(F32)
+
+    y_order = [n - nx for n in range(whole, tiles)] + list(range(whole - nx))
+    x_order = [h * hx + j for j in range(hx) for h in range(2)]
+    order = [nx + i for i in y_order] + x_order
+
     def last_weights(p):
-        def put(n):
+        for n in order:
             total = (acc[n] + tile(p, n)).astype(BF16)
             stage[n] = total.reshape(stage.shape[1:])
             give_twin(n).start()
 
-        for n in range(whole, tiles):
-            put(n)
-
-        def qkv(i):
-            put(whole - 1 - i)
-
-        loop(whole, qkv)
-
-    def join(at, other):
-        stage[at] = (stage[at].astype(F32) + other.astype(F32)).astype(BF16)
+            @pl.when(core == 0)
+            def _():
+                arrive(n)
 
     def reduce_out():
-        nx, ny = TX, tiles - TX
-        hx, hy = nx // 2, ny // 2
-        xa, xb = pl.ds(0, hx), pl.ds(hx, nx - hx)
-        ya, yb = pl.ds(nx, hy), pl.ds(nx + hy, ny - hy)
-        base = tiles
-        y1 = [
-            send(stage.at[nx + i, :, 1 - row, core], got_y1.at[i], base + i, to_row)
-            for i in range(ny)
-        ]
-        base += ny
-        x1 = (
-            send(stage.at[xa, far, :, core], got_x1.at[0, 0:hx], base, to_right),
-            send(stage.at[xb, far, :, core], got_x1.at[1, 0 : nx - hx], base + 1, to_left),
-        )
-        x2a = (
-            send(stage.at[xb, right, :, core], got_x2.at[0, hx:nx], base + 2, to_right),
-            send(stage.at[xa, left, :, core], got_x2.at[1, 0:hx], base + 3, to_left),
-        )
-        x2b = (
-            send(stage.at[xa, right, :, core], got_x2.at[0, 0:hx], base + 4, to_right),
-            send(stage.at[xb, left, :, core], got_x2.at[1, hx:nx], base + 5, to_left),
-        )
-        y2 = (
-            send(stage.at[ya, far, row, core], got_y2.at[0, 0:hy], base + 6, to_right),
-            send(stage.at[yb, far, row, core], got_y2.at[1, 0 : ny - hy], base + 7, to_left),
-        )
-        y3a = (
-            send(stage.at[yb, right, row, core], got_y3.at[0, hy:ny], base + 8, to_right),
-            send(stage.at[ya, left, row, core], got_y3.at[1, 0:hy], base + 9, to_left),
-        )
-        y3b = (
-            send(stage.at[ya, right, row, core], got_y3.at[0, 0:hy], base + 10, to_right),
-            send(stage.at[yb, left, row, core], got_y3.at[1, hy:ny], base + 11, to_left),
-        )
-        x3 = send(send_x3, got_x3, base + 12, to_row)
-
-        def meet(n):
-            give_twin(n).wait_recv()
-            for c in range(cols):
-                join((n, c, slice(None), core), got_a[n, c])
-
-        for i in reversed(range(ny)):
-            meet(nx + i)
-            y1[i].start()
-
-        def meet_x(i):
-            meet(nx - 1 - i)
-
-        loop(nx, meet_x)
-        for copy in x1 + x2a:
-            copy.start()
+        @pl.when(core == 1)
+        def _():
+            for n in order:
+                arrive(n)
+
+        pairs = [x_order[2 * j : 2 * j + 2] for j in range(hx)]
+        for n in pairs[0]:
+            x_second(n)
+        y_first(y_order[0])
+        for n in pairs[1]:
+            x_second(n)
+        y_first(y_order[1])
+        for n in pairs[2]:
+            x_second(n)
+        y_second(y_order[0])
+        y_first(y_order[2])
+        y_second(y_order[1])
+        for n in pairs[0]:
+            x_third(n)
+        y_first(y_order[3])
+        y_second(y_order[2])
+        for n in pairs[1]:
+            x_third(n)
+        y_second(y_order[3])
+        for n in pairs[2]:
+            x_third(n)
+        for i in y_order:
+            y_last(i)
+        for n in x_order:
+            x_last(n)
+        for n in range(tiles):
+            give_twin(n).wait_send()
+        for n in range(nx):
+            for copy in (copy_x1(n), copy_x2(0, n), copy_x2(1, n), copy_x3(n)):
+                copy.wait_send()
         for i in range(ny):
-            y1[i].wait_recv()
-            for c in range(cols):
-                join((nx + i, c, row, core), got_y1[i, c])
-        x1[0].wait_recv()
-        for i in range(hx):
-            join((i, right, slice(None), core), got_x1[0, i])
-        x2b[0].start()
-        x1[1].wait_recv()
-        for i in range(nx - hx):
-            join((hx + i, left, slice(None), core), got_x1[1, i])
-        x2b[1].start()
-        for copy in y2 + y3a:
-            copy.start()
-        y2[0].wait_recv()
-        for i in range(hy):
-            join((nx + i, right, row, core), got_y2[0, i])
-        y3b[0].start()
-        y2[1].wait_recv()
-        for i in range(ny - hy):
-            join((nx + hy + i, left, row, core), got_y2[1, i])
-        y3b[1].start()
-
-        def across(n, r):
-            total = stage[n, col, r, core].astype(F32) + got_x2[0, n, r].astype(F32)
-            return total + got_x2[1, n, r].astype(F32)
-
-        for copy in x2a + x2b:
-            copy.wait_recv()
-        for n in range(nx):
-            send_x3[n] = across(n, 1 - row).astype(BF16)
-        x3.start()
-
-        def emit(n, value):
-            if n < whole:
-                qkv_out[:, n * TILE : (n + 1) * TILE] = value
-            elif n == whole:
-                qkv_out[:, n * TILE : packed] = value[:, : TILE - edge]
-                out_out[:, 0:edge] = value[:, TILE - edge :]
-            else:
-                start = edge + (n - whole - 1) * TILE
-                out_out[:, start : start + TILE] = value
-
-        for copy in y3a + y3b:
-            copy.wait_recv()
-        for i in range(ny):
-            total = stage[nx + i, col, row, core].astype(F32) + got_y3[0, i].astype(F32)
-            emit(nx + i, total + got_y3[1, i].astype(F32))
-        x3.wait_recv()
-        for n in range(nx):
-            emit(n, across(n, row) + got_x3[n].astype(F32))
-        for copy in tuple(y1) + x1 + x2a + x2b + y2 + y3a + y3b + (x3,):
-            copy.wait_send()
-
-        def given(n):
-            give_twin(n).wait_send()
-
-        loop(tiles, given)
+            for copy in (copy_y1(i), copy_y2(i), copy_y3(0, i), copy_y3(1, i)):
+                copy.wait_send()
 
     def clear(c):
         acc[:, rows_at(c, 32), :] = jnp.zeros((tiles, 32, TILE), F32)
@@ -578,17 +594,14 @@
         pltpu.VMEM((2, tiles - TX, share, TILE), BF16),
         pltpu.VMEM((TX, share, TILE), BF16),
         pltpu.VMEM((TX, share, TILE), BF16),
-        pltpu.SemaphoreType.DMA((tiles + tiles - TX + 13,)),
-        pltpu.SemaphoreType.DMA((tiles + tiles - TX + 13,)),
+        pltpu.SemaphoreType.DMA((tiles + 4 * TX + 4 * (tiles - TX),)),
+        pltpu.SemaphoreType.DMA((tiles + 4 * TX + 4 * (tiles - TX),)),
     ]
     return pl.pallas_call(
         functools.partial(pipeline_kernel, sections),
-        out_shape=(
-            jax.ShapeDtypeStruct((share, packed), F32),
-            jax.ShapeDtypeStruct((share, head_span), F32),
-        ),
+        out_shape=jax.ShapeDtypeStruct((share, packed + head_span), F32),
         in_specs=[smem, smem, hbm, hbm, vmem, hbm, hbm],
-        out_specs=(vmem, vmem),
+        out_specs=vmem,
         scratch_shapes=scratch,
         compiler_params=pltpu.CompilerParams(
             collective_id=0, has_side_effects=True, vmem_limit_bytes=64 * 1024 * 1024 - 65536
@@ -597,9 +610,16 @@
     )(counts, arrival, x, cotangent, gain, wqkv, wo)
 
 
+def split_kernel(both_ref, qkv_ref, out_ref):
+    packed = qkv_ref.shape[1]
+    qkv_ref[...] = both_ref[:, :packed]
+    out_ref[...] = both_ref[:, packed:]
+
+
 def per_device(activations, cotangent, counts, arrival, norm_gain, qkv_weight, out_weight):
     sections = lax.axis_size("section")
-    qkv_share, out_share = run_pipeline(
+    packed = qkv_weight.shape[2]
+    both = run_pipeline(
         sections,
         lax.axis_size("dp"),
         counts[:, 0],
@@ -610,6 +630,18 @@
         qkv_weight[0],
         out_weight[0],
     )
+    share, width = both.shape
+    vmem = pl.BlockSpec(memory_space=pltpu.VMEM)
+    qkv_share, out_share = pl.pallas_call(
+        split_kernel,
+        out_shape=(
+            jax.ShapeDtypeStruct((share, packed), F32),
+            jax.ShapeDtypeStruct((share, width - packed), F32),
+        ),
+        in_specs=[vmem],
+        out_specs=(vmem, vmem),
+        name="split",
+    )(both)
     return (qkv_share[None], out_share[None])
 
 

time: 207 us -> 202 us (0.976); the launches traced: 203 us -> 202 us
  local copies, waits for them, and re-layouts: 3.56 us -> 0 us
    unnamed x2 -> x0, local copies, waits for them, and re-layouts: 3.56 us -> none
    pallas_call x1 -> x2, Pallas kernels: 199 us -> 201 us  [the longest x1 199 us: run_pipeline(): pl.pallas_call(functools.partial(pipeline_kernel, sections), out_shape=ja...]
where the time goes in v5:
time: 202 us
  Pallas kernels  201 us (100%)
    pallas_call x1, Pallas kernels, run_pipeline(): pl.pallas_call(functools.partial(pipeline_kernel, sections), out_shape=ja...  199 us

profile of v5, /device:TPU:1, one launch (start us, length us, event | category | flops | bytes accessed | tf_op | source)
XLA Modules:
  0.0 202.0 jit_solution(2468956156209888137)
XLA Ops:
  0.6 199.3 %pipeline.1.both_ref = f32[80,2560]{1,0:T(8,128)} custom-call(s32[4]{0:T(128)} %bitcast.9, s32[4]{0:T(128)} %arrival_ref.1, bf16[4,256,1280]{2,1,0:T(8,128)(2,1)} %bitcast.7, bf16[4,256,1280]{2,1,0:T(8,128)(2,1)} %cot_hbm.1, f32[1,1280]{1,0:T(1,128)} %gain_ref.1, bf16[1280,1920]{1,0:T(8,128)(2,1)} %bitcast.6, bf16[1280,640]{1,0:T(8,128)(2,1)} %bitcast.8), custom_call_target="tpu_custom_call" | custom-call | tf_op jit(solution)/shard_map/pipeline/pallas_call | solution.py:600
  199.9 2.1 %split.1 = (f32[80,1920]{1,0:T(8,128)}, f32[80,640]{1,0:T(8,128)}) custom-call(f32[80,2560]{1,0:T(8,128)} %pipeline.1.both_ref), custom_call_target="tpu_custom_call" | custom-call | tf_op jit(solution)/shard_map/split/pallas_call | solution.py:635

commit v6 on v5

--- a/solution.py
+++ b/solution.py
@@ -14,7 +14,7 @@
 TILE = 256
 PIECE = 256
 TX = 6
-TURN = 2
+TURN = 3
 F32 = jnp.float32
 BF16 = jnp.bfloat16
 
@@ -147,7 +147,6 @@
         pl.semaphore_signal(barrier, inc=1, device_id={"section": other}, device_id_type=MESH)
     for other in (twin, to_right, to_left, to_row):
         pl.semaphore_signal(barrier, inc=1, device_id={"dp": other}, device_id_type=MESH)
-    pl.semaphore_wait(barrier, 6)
     gain_b[...] = jnp.broadcast_to(gain_ref[...], (128, width)).T
     load_x.wait()
 
@@ -158,15 +157,13 @@
         for i, (at, size) in enumerate(wo_parts):
             load_wo[i].wait()
             wo_t[at : at + size, :] = hid_t[1 + i, :, 0:size].T
-        gain_hi = gain_b[...].astype(BF16)
-        gain_lo = (gain_b[...] - gain_hi.astype(F32)).astype(BF16)
-        gains = jnp.concatenate([gain_hi, gain_lo], axis=1)
-
-        def weigh(m):
-            both = dot_nn(wqkv_t[rows_at(m, 480), :], gains) * (1.0 / width)
-            gain_w[rows_at(m, 480), :] = both[:, :128] + both[:, 128:]
-
-        loop(packed // 480, weigh)
+        gains = jnp.broadcast_to(gain_ref[...], (16, width))
+        high = gains.astype(BF16).astype(F32)
+        at_row = lax.broadcasted_iota(jnp.int32, (16, width), 0)
+        gains = jnp.where(at_row == 0, high, jnp.where(at_row == 1, gains - high, 0.0))
+        sums = dot_nn(gains.astype(BF16), wqkv_ref[...])
+        sums = jnp.sum(sums, axis=0, keepdims=True) * (1.0 / width)
+        gain_w[...] = jnp.broadcast_to(sums, (128, packed)).T
 
     CH = 160
     chunks = width // CH
@@ -390,13 +387,13 @@
             join((n, c, slice(None), core), got_a[n, c])
         if n < nx:
             copy_x1(n).start()
-            copy_x2(1 - n // hx, n).start()
         else:
             copy_y1(n - nx).start()
 
     def x_second(n):
         way = n // hx
         copy_x1(n).wait_recv()
+        copy_x2(1 - way, n).start()
         join((n, ways[way][1], slice(None), core), got_x1[way, n % hx])
         copy_x2(way, n).start()
 
@@ -504,6 +501,7 @@
         return carry
 
     lax.fori_loop(0, ahead, early, 0)
+    pl.semaphore_wait(barrier, 6)
 
     def moment(p):
         sums = backward(p)

time: 202 us -> 202 us (level)
  no operation moved by 1% of the time
where the time goes in v6:
time: 202 us
  Pallas kernels  201 us (100%)
    pallas_call x1, Pallas kernels, run_pipeline(): pl.pallas_call(functools.partial(pipeline_kernel, sections), out_shape=ja...  199 us

profile of v6, /device:TPU:1, one launch (start us, length us, event | category | flops | bytes accessed | tf_op | source)
XLA Modules:
  0.0 201.8 jit_solution(11459416142649405637)
XLA Ops:
  0.6 199.1 %pipeline.1.both_ref = f32[80,2560]{1,0:T(8,128)} custom-call(s32[4]{0:T(128)} %bitcast.9, s32[4]{0:T(128)} %arrival_ref.1, bf16[4,256,1280]{2,1,0:T(8,128)(2,1)} %bitcast.7, bf16[4,256,1280]{2,1,0:T(8,128)(2,1)} %cot_hbm.1, f32[1,1280]{1,0:T(1,128)} %gain_ref.1, bf16[1280,1920]{1,0:T(8,128)(2,1)} %bitcast.6, bf16[1280,640]{1,0:T(8,128)(2,1)} %bitcast.8), custom_call_target="tpu_custom_call" | custom-call | tf_op jit(solution)/shard_map/pipeline/pallas_call | solution.py:598
  199.8 2.1 %split.1 = (f32[80,1920]{1,0:T(8,128)}, f32[80,640]{1,0:T(8,128)}) custom-call(f32[80,2560]{1,0:T(8,128)} %pipeline.1.both_ref), custom_call_target="tpu_custom_call" | custom-call | tf_op jit(solution)/shard_map/split/pallas_call | solution.py:633

commit v7 on v6

--- a/solution.py
+++ b/solution.py
@@ -14,7 +14,7 @@
 TILE = 256
 PIECE = 256
 TX = 6
-TURN = 3
+TURN = 2
 F32 = jnp.float32
 BF16 = jnp.bfloat16
 

time: 202 us -> 201 us (level)
  no operation moved by 1% of the time
where the time goes in v7:
time: 201 us
  Pallas kernels  200 us (100%)
    pallas_call x1, Pallas kernels, run_pipeline(): pl.pallas_call(functools.partial(pipeline_kernel, sections), out_shape=ja...  198 us

profile of v7, /device:TPU:1, one launch (start us, length us, event | category | flops | bytes accessed | tf_op | source)
XLA Modules:
  0.0 200.8 jit_solution(2142657910119185706)
XLA Ops:
  0.6 198.1 %pipeline.1.both_ref = f32[80,2560]{1,0:T(8,128)} custom-call(s32[4]{0:T(128)} %bitcast.9, s32[4]{0:T(128)} %arrival_ref.1, bf16[4,256,1280]{2,1,0:T(8,128)(2,1)} %bitcast.7, bf16[4,256,1280]{2,1,0:T(8,128)(2,1)} %cot_hbm.1, f32[1,1280]{1,0:T(1,128)} %gain_ref.1, bf16[1280,1920]{1,0:T(8,128)(2,1)} %bitcast.6, bf16[1280,640]{1,0:T(8,128)(2,1)} %bitcast.8), custom_call_target="tpu_custom_call" | custom-call | tf_op jit(solution)/shard_map/pipeline/pallas_call | solution.py:598
  198.7 2.1 %split.1 = (f32[80,1920]{1,0:T(8,128)}, f32[80,640]{1,0:T(8,128)}) custom-call(f32[80,2560]{1,0:T(8,128)} %pipeline.1.both_ref), custom_call_target="tpu_custom_call" | custom-call | tf_op jit(solution)/shard_map/split/pallas_call | solution.py:633
